TPU v7x, 32 devices: a whole 2x2x4 slice. The times are simulated.
32 devices in a mesh: fsdp: 16 (over z, x, core), tp: 2 (over y).
Axes of the slice: x: 2, y: 2, z: 4, core: 2. Of those that a mesh axis runs over, the one named last changes fastest.
Arguments:
- frames: bfloat16 [16, 1536, 1280], P('fsdp', 'tp'), may hold values from -6 to 6
- cotangent: bfloat16 [16, 1536, 1280], P('fsdp', 'tp'), may hold values from -6 to 6
- w_query: bfloat16 [1280, 1280], P('fsdp', 'tp'), may hold values from -0.3689512 to 0.3689512
- w_key: bfloat16 [1280, 1280], P('fsdp', 'tp'), may hold values from -0.15625 to 0.15625
- w_value: bfloat16 [1280, 1280], P('fsdp', 'tp'), may hold values from -0.15625 to 0.15625
- w_output: bfloat16 [1280, 1280], P('tp', 'fsdp'), may hold values from -1 to 1
- w_up: bfloat16 [1280, 5120], P('fsdp', 'tp'), may hold values from -0.15625 to 0.15625
- w_down: bfloat16 [5120, 1280], P('tp', 'fsdp'), may hold values from -0.078125 to 0.078125
- norm_gains: float32 [2, 1280], replicated, may hold values from 0.1 to 1.9
- norm_biases: float32 [2, 1280], replicated, may hold values from -3 to 3
- clip_lengths: int32 [16], replicated, may hold values from 160 to 1500, as said below
- clip_slot: int32 [16], replicated, may hold values from 0 to 15, each once
Outputs:
- output_frames: bfloat16 [16, 1536, 1280], P('fsdp', 'tp')
- grad_frames: float32 [16, 1536, 1280], P('fsdp', 'tp')
- grad_query: float32 [1280, 1280], P('fsdp', 'tp')
- grad_key: float32 [1280, 1280], P('fsdp', 'tp')
- grad_value: float32 [1280, 1280], P('fsdp', 'tp')
- grad_output: float32 [1280, 1280], P('tp', 'fsdp')
- grad_up: float32 [1280, 5120], P('fsdp', 'tp')
- grad_down: float32 [5120, 1280], P('tp', 'fsdp')
- grad_gains: float32 [2, 1280], replicated
- grad_biases: float32 [2, 1280], replicated
- scaled_query: float32 [1280, 1280], P('fsdp', 'tp')
- scaled_key: float32 [1280, 1280], P('fsdp', 'tp')
Inputs may be any that keep to these rules, and one draw needn't show every extreme that they name: `clip_lengths`: one clip has exactly 1500 live frames. `clip_slot`: slot s lies on index s // 1 of fsdp.
All inputs are finite; a program needn't handle non-finite values.
Results may differ from a plain program's by a relative error of at most 0.02.
Values may be sent and summed in bfloat16 or wider, within the bound.
A program may use at most 256 MiB of HBM per device.

v0:
```python
import functools
import math

import jax
import jax.numpy as jnp
from jax import lax
from jax.experimental import pallas as pl
from jax.experimental.pallas import tpu as pltpu
from jax.sharding import PartitionSpec as P


HEAD_DIM = 80
LANES = 128
NORM_EPSILON = 1e-05
CLIP_LIMIT = 6.0
MASK_FILL = -1e30
SCORE_SCALE = HEAD_DIM**-0.5
SCALE_LOG2 = SCORE_SCALE * math.log2(math.e)
VMEM_BYTES = 60 * 2**20
LOW = jnp.bfloat16
WIDE = jnp.float32


def split_three(column):
    high = column.astype(LOW)
    rest = column - high.astype(WIDE)
    middle = rest.astype(LOW)
    return high, middle, (rest - middle.astype(WIDE)).astype(LOW)


def gather_head(pieces, target):
    place = 0
    for piece in pieces:
        width = piece.shape[1]
        target[:HEAD_DIM, place : place + width] = piece[...]
        place += width


def live_frames(shape, info_ref):
    place = lax.broadcasted_iota(jnp.int32, shape, 1) + info_ref[1]
    place = jnp.where(place >= info_ref[2], place - info_ref[2], place)
    return place < info_ref[0]


def dead_lane(info_ref, width):
    return jnp.where(live_frames((1, width), info_ref), 0.0, MASK_FILL)


def whole_block(shape):
    return pl.BlockSpec(shape, lambda *_: (0,) * len(shape))


def head_block(width, first):
    return pl.BlockSpec((HEAD_DIM, width), lambda head, *_: (head + first, 0))


def forward_kernel(parts, info_ref, *refs):
    q_pieces, k_pieces, v_pieces = (refs[n * parts : (n + 1) * parts] for n in range(3))
    out_ref, total_ref, top_ref, q_t, k_t, v_t = refs[3 * parts :]
    head = pl.program_id(0)
    width = q_t.shape[1]

    @pl.when(head == 0)
    def _():
        row = lax.broadcasted_iota(jnp.int32, (LANES, width), 0)
        q_t[...] = jnp.where(row == HEAD_DIM, 1.0, 0.0).astype(LOW)
        k_t[...] = jnp.where(row == HEAD_DIM, dead_lane(info_ref, width), 0.0).astype(LOW)

    gather_head(q_pieces, q_t)
    gather_head(k_pieces, k_t)
    gather_head(v_pieces, v_t)
    scores = jnp.dot(k_t[...].T, q_t[...], preferred_element_type=WIDE)
    top = jnp.max(scores, axis=0, keepdims=True)
    weights = jnp.exp2((scores - top) * SCALE_LOG2)
    total = jnp.sum(weights, axis=0, keepdims=True)
    mixed = jnp.dot(v_t[...], weights.astype(LOW), preferred_element_type=WIDE)
    out_ref[...] = (mixed * (1.0 / total)).astype(LOW)
    total_ref[pl.ds(head, 1), :] = top + jnp.log2(total) * (1.0 / SCALE_LOG2)
    live_top = jnp.where(live_frames((1, width), info_ref), top, MASK_FILL)
    live_top = jnp.max(live_top, axis=1, keepdims=True)
    top_ref[pl.ds(head, 1), :] = jnp.broadcast_to(live_top, (1, LANES))


def attention_forward(pieces, info, first_head, count):
    width = sum(piece.shape[1] for piece in pieces)
    heads = pieces[0].shape[0] // (3 * HEAD_DIM)
    return pl.pallas_call(
        functools.partial(forward_kernel, len(pieces)),
        out_shape=(
            jax.ShapeDtypeStruct((count * HEAD_DIM, width), LOW),
            jax.ShapeDtypeStruct((count, width), WIDE),
            jax.ShapeDtypeStruct((count, LANES), WIDE),
        ),
        grid_spec=pltpu.PrefetchScalarGridSpec(
            num_scalar_prefetch=1,
            grid=(count,),
            in_specs=[
                head_block(piece.shape[1], first_head + n * heads)
                for n in range(3)
                for piece in pieces
            ],
            out_specs=[
                head_block(width, 0),
                whole_block((count, width)),
                whole_block((count, LANES)),
            ],
            scratch_shapes=[pltpu.VMEM((LANES, width), LOW)] * 2
            + [pltpu.VMEM((HEAD_DIM, width), LOW)],
        ),
        compiler_params=pltpu.CompilerParams(vmem_limit_bytes=VMEM_BYTES),
        name="attention_forward",
        cost_estimate=pl.CostEstimate(
            flops=14 * count * width * width * LANES,
            transcendentals=count * width * width,
            bytes_accessed=8 * width * count * HEAD_DIM,
        ),
    )(info, *pieces, *pieces, *pieces)


def backward_kernel(parts, info_ref, *refs):
    q_pieces, k_pieces, v_pieces, g_pieces = (
        refs[n * parts : (n + 1) * parts] for n in range(4)
    )
    att_ref, total_ref, out_ref, q_t, k_t, v_t, g_t = refs[4 * parts :]
    head = pl.program_id(0)
    width = q_t.shape[1]
    extra = HEAD_DIM + 1

    @pl.when(head == 0)
    def _():
        row = lax.broadcasted_iota(jnp.int32, (LANES, width), 0)
        ones = jnp.where((row >= extra) & (row < extra + 3), 1.0, 0.0)
        q_t[...] = jnp.where(row == HEAD_DIM, 1.0, 0.0).astype(LOW)
        k_t[...] = jnp.where(row == HEAD_DIM, dead_lane(info_ref, width), ones).astype(LOW)
        v_t[...] = ones.astype(LOW)
        g_t[...] = jnp.zeros_like(g_t)

    gather_head(q_pieces, q_t)
    gather_head(k_pieces, k_t)
    gather_head(v_pieces, v_t)
    gather_head(g_pieces, g_t)
    for index, part in enumerate(split_three(-total_ref[pl.ds(head, 1), :])):
        q_t[extra + index : extra + index + 1, :] = part
    inner = jnp.sum(
        att_ref[...].astype(WIDE) * g_t[:HEAD_DIM, :].astype(WIDE), axis=0, keepdims=True
    )
    for index, part in enumerate(split_three(-inner)):
        g_t[extra + index : extra + index + 1, :] = part

    queries = q_t[...]
    grads = g_t[...]
    scores = jnp.dot(k_t[...].T, queries, preferred_element_type=WIDE)
    weights = jnp.exp2(scores * SCALE_LOG2)
    grad_weights = jnp.dot(v_t[...].T, grads, preferred_element_type=WIDE)
    grad_scores = (weights * grad_weights).astype(LOW)
    grad_v = jnp.dot(weights.astype(LOW), grads.T, preferred_element_type=WIDE)
    grad_k = jnp.dot(grad_scores, queries.T, preferred_element_type=WIDE)
    grad_q = jnp.dot(k_t[:HEAD_DIM, :], grad_scores, preferred_element_type=WIDE)
    out_ref[0] = (grad_q * SCORE_SCALE).astype(LOW)
    out_ref[1] = (grad_k.T[:HEAD_DIM] * SCORE_SCALE).astype(LOW)
    out_ref[2] = grad_v.T[:HEAD_DIM].astype(LOW)


def attention_backward(pieces, attended, grad_pieces, totals, info, first_head):
    group, width = attended.shape
    count = group // HEAD_DIM
    heads = pieces[0].shape[0] // (3 * HEAD_DIM)
    grads = pl.pallas_call(
        functools.partial(backward_kernel, len(pieces)),
        out_shape=jax.ShapeDtypeStruct((3, group, width), LOW),
        grid_spec=pltpu.PrefetchScalarGridSpec(
            num_scalar_prefetch=1,
            grid=(count,),
            in_specs=[
                head_block(piece.shape[1], first_head + n * heads)
                for n in range(3)
                for piece in pieces
            ]
            + [head_block(piece.shape[1], first_head) for piece in grad_pieces]
            + [head_block(width, 0), whole_block(totals.shape)],
            out_specs=pl.BlockSpec((3, HEAD_DIM, width), lambda head, *_: (0, head, 0)),
            scratch_shapes=[pltpu.VMEM((LANES, width), LOW)] * 4,
        ),
        compiler_params=pltpu.CompilerParams(vmem_limit_bytes=VMEM_BYTES),
        name="attention_backward",
        cost_estimate=pl.CostEstimate(
            flops=26 * count * width * width * LANES,
            transcendentals=count * width * width,
            bytes_accessed=16 * width * count * HEAD_DIM,
        ),
    )(info, *pieces, *pieces, *pieces, *grad_pieces, attended, totals)
    return grads.reshape(3 * group, width)


def split_place(fsdp):
    inner = 2 if fsdp % 2 == 0 else 1
    middle = 2 if fsdp % (2 * inner) == 0 else 1
    return fsdp // (inner * middle), middle, inner


def gather_kernel(fsdp, tp, shard_qkv, shard_out, frames_ref, *refs):
    qkv_ref, out_ref, others_ref, own_sem, sent, got, tp_sent, tp_got = refs
    outer, middle, inner = split_place(fsdp)
    spot = lax.axis_index("fsdp")
    rank = lax.axis_index("tp")
    core = lax.rem(spot, inner)
    side = lax.rem(lax.div(spot, inner), middle)
    line = lax.div(spot, inner * middle)

    def at(step_line, step_side, step_core):
        new_line = lax.rem(line + outer - step_line, outer)
        new_side = lax.rem(side + middle - step_side, middle)
        new_core = lax.rem(core + inner - step_core, inner)
        return (new_line * middle + new_side) * inner + new_core

    lines = [at(outer - step, 0, 0) for step in range(1, outer)]
    sides = [at(0, middle - step, 0) for step in range(1, middle)]
    cores = [at(0, 0, inner - step) for step in range(1, inner)]
    ranks = [lax.rem(rank + step, tp) for step in range(1, tp)]
    barrier = pltpu.get_barrier_semaphore()
    for peer in (*lines, *sides, *cores):
        pl.semaphore_signal(
            barrier, inc=1, device_id={"fsdp": peer}, device_id_type=pl.DeviceIdType.MESH
        )
    for peer in ranks:
        pl.semaphore_signal(
            barrier, inc=1, device_id={"tp": peer}, device_id_type=pl.DeviceIdType.MESH
        )
    pl.semaphore_wait(barrier, len(lines) + len(sides) + len(cores) + len(ranks))

    started = []

    def send(source, target, send_sem, recv_sem, axis, peer):
        copy = pltpu.make_async_remote_copy(
            src_ref=source,
            dst_ref=target,
            send_sem=send_sem,
            recv_sem=recv_sem,
            device_id={axis: peer},
            device_id_type=pl.DeviceIdType.MESH,
        )
        copy.start()
        started.append(copy)

    def arrived(target, recv_sem):
        pltpu.make_async_remote_copy(
            src_ref=target,
            dst_ref=target,
            send_sem=recv_sem,
            recv_sem=recv_sem,
            device_id={"tp": ranks[0] if ranks else rank},
            device_id_type=pl.DeviceIdType.MESH,
        ).wait_recv()

    for step in range(1, tp):
        send(
            shard_out,
            out_ref.at[tp - step, spot],
            tp_sent.at[0, step - 1],
            tp_got.at[0, step - 1],
            "tp",
            ranks[step - 1],
        )
    own_qkv = pltpu.make_async_copy(shard_qkv, qkv_ref.at[spot], own_sem.at[0])
    own_out = pltpu.make_async_copy(shard_out, out_ref.at[0, spot], own_sem.at[1])
    own_qkv.start()
    own_out.start()
    for step in range(1, tp):
        send(
            frames_ref,
            others_ref.at[tp - step - 1],
            tp_sent.at[1, step - 1],
            tp_got.at[1, step - 1],
            "tp",
            ranks[step - 1],
        )

    def forward(kind, block, source, step_line, step_side, number):
        index = number
        if step_line == 0 and step_side == 0:
            for step, peer in enumerate(lines):
                send(source, block, sent.at[kind, index], got.at[kind, 0, step + 1], "fsdp", peer)
                index += 1
        if step_side == 0:
            for step, peer in enumerate(sides):
                slot = (step + 1) * outer + step_line
                send(source, block, sent.at[kind, index], got.at[kind, 0, slot], "fsdp", peer)
                index += 1
        for step, peer in enumerate(cores):
            slot = step_side * outer + step_line
            send(source, block, sent.at[kind, index], got.at[kind, step + 1, slot], "fsdp", peer)
            index += 1
        return index

    def block_of_kind(kind, place):
        return qkv_ref.at[place] if kind == 0 else out_ref.at[:, place]

    counts = [0, 0]
    counts[0] = forward(0, qkv_ref.at[spot], shard_qkv, 0, 0, 0)
    own_out.wait()
    for step in range(1, tp):
        arrived(out_ref.at[tp - step, spot], tp_got.at[0, step - 1])
    counts[1] = forward(1, out_ref.at[:, spot], out_ref.at[:, spot], 0, 0, 0)
    for step_side in range(middle):
        for kind in range(2):
            for step_line in range(outer):
                if step_line == 0 and step_side == 0:
                    continue
                block = block_of_kind(kind, at(step_line, step_side, 0))
                arrived(block, got.at[kind, 0, step_side * outer + step_line])
                counts[kind] = forward(kind, block, block, step_line, step_side, counts[kind])
    for kind in range(2):
        for step in range(1, inner):
            for step_side in range(middle):
                for step_line in range(outer):
                    block = block_of_kind(kind, at(step_line, step_side, step))
                    arrived(block, got.at[kind, step, step_side * outer + step_line])
    for step in range(1, tp):
        arrived(others_ref.at[tp - step - 1], tp_got.at[1, step - 1])
    own_qkv.wait()
    for copy in started:
        copy.wait_send()


def gather_start(shard_qkv, shard_out, frames, fsdp):
    tp = lax.axis_size("tp")
    rows, cols = shard_out.shape
    outer, middle, inner = split_place(fsdp)
    sends = (outer - 1) + (middle - 1) * outer + (inner - 1) * outer * middle
    anywhere = pl.BlockSpec(memory_space=pl.ANY)
    return pl.pallas_call(
        functools.partial(gather_kernel, fsdp, tp),
        out_shape=(
            jax.ShapeDtypeStruct((fsdp, rows, 3 * cols), LOW),
            jax.ShapeDtypeStruct((tp, fsdp, rows, cols), LOW),
            jax.ShapeDtypeStruct((tp - 1, *frames.shape), LOW),
        ),
        in_specs=[anywhere] * 3,
        out_specs=[anywhere] * 3,
        scratch_shapes=[
            pltpu.SemaphoreType.DMA((2,)),
            pltpu.SemaphoreType.DMA((2, sends)),
            pltpu.SemaphoreType.DMA((2, inner, middle * outer)),
            pltpu.SemaphoreType.DMA((2, tp - 1)),
            pltpu.SemaphoreType.DMA((2, tp - 1)),
        ],
        compiler_params=pltpu.CompilerParams(collective_id=0, has_side_effects=True),
        name="gather_start",
        cost_estimate=pl.CostEstimate(
            flops=0, transcendentals=0, bytes_accessed=8 * fsdp * rows * cols
        ),
    )(shard_qkv, shard_out, frames)


def merge_rows(left, right):
    row = lax.broadcasted_iota(jnp.int32, left.shape, 0)
    return jnp.where(row < 4, left + right, jnp.maximum(left, right))


def scatter_kernel(fsdp, tp, count, *refs):
    parts = refs[:count]
    small_ref = refs[count]
    outs = refs[count + 1 : 2 * count + 1 - (tp - 1)]
    small_out = refs[2 * count + 1 - (tp - 1)]
    scratch = refs[2 * count + 2 - (tp - 1) :]
    from_core, sum_core, from_side, sum_side, from_line, wide = (
        scratch[n * count : (n + 1) * count] for n in range(6)
    )
    (
        to_rank,
        from_rank,
        small_sum,
        small_got,
        core_sem,
        side_sem,
        line_sem,
        rank_sem,
        small_sem,
    ) = scratch[6 * count :]
    outer, middle, inner = split_place(fsdp)
    spot = lax.axis_index("fsdp")
    rank = lax.axis_index("tp")
    core = lax.rem(spot, inner)
    side = lax.rem(lax.div(spot, inner), middle)
    line = lax.div(spot, inner * middle)

    def at(new_line, new_side, new_core):
        return (new_line * middle + new_side) * inner + new_core

    core_steps = [lax.rem(core + step, inner) for step in range(1, inner)]
    side_steps = [lax.rem(side + step, middle) for step in range(1, middle)]
    line_steps = [lax.rem(line + step, outer) for step in range(1, outer)]
    cores = [at(line, side, item) for item in core_steps]
    sides = [at(line, item, core) for item in side_steps]
    lines = [at(item, side, core) for item in line_steps]
    ranks = [lax.rem(rank + step, tp) for step in range(1, tp)]
    barrier = pltpu.get_barrier_semaphore()
    for peer in (*lines, *sides, *cores):
        pl.semaphore_signal(
            barrier, inc=1, device_id={"fsdp": peer}, device_id_type=pl.DeviceIdType.MESH
        )
    for peer in ranks:
        pl.semaphore_signal(
            barrier, inc=1, device_id={"tp": peer}, device_id_type=pl.DeviceIdType.MESH
        )
    pl.semaphore_wait(barrier, len(lines) + len(sides) + len(cores) + len(ranks))

    def send(source, target, sems, axis, peer):
        copy = pltpu.make_async_remote_copy(
            src_ref=source,
            dst_ref=target,
            send_sem=sems.at[0],
            recv_sem=sems.at[1],
            device_id={axis: peer},
            device_id_type=pl.DeviceIdType.MESH,
        )
        copy.start()
        return copy

    small_copies = []

    def small_stage(first, axis, peers, source):
        for index, peer in enumerate(peers):
            number = first + index
            small_copies.append(
                send(source, small_got.at[number], small_sem.at[number], axis, peer)
            )

    def small_merge(first, peers, current, merge):
        for index in range(len(peers)):
            small_copies[first + index].wait_recv()
            current = merge(current, small_got[first + index])
        return current

    small_stage(0, "fsdp", cores, small_ref)
    core_copies = [
        [
            send(
                part.at[:, core_steps[step]],
                from_core[index].at[step],
                core_sem.at[index, step],
                "fsdp",
                cores[step],
            )
            for step in range(inner - 1)
        ]
        for index, part in enumerate(parts)
    ]
    total = small_merge(0, cores, small_ref[...], merge_rows)
    small_sum[0] = total
    first_small = len(cores)
    small_stage(first_small, "fsdp", sides, small_sum.at[0])

    side_copies = []
    for index, part in enumerate(parts):
        for copy in core_copies[index]:
            copy.wait_recv()

        def add_core(n, carry, index=index, part=part):
            value = part[n, core].astype(WIDE)
            for step in range(inner - 1):
                value = value + from_core[index][step, n].astype(WIDE)
            sum_core[index][lax.div(n, middle), lax.rem(n, middle)] = value.astype(LOW)
            return carry

        lax.fori_loop(0, outer * middle, add_core, 0)
        side_copies.append(
            [
                send(
                    sum_core[index].at[:, side_steps[step]],
                    from_side[index].at[step],
                    side_sem.at[index, step],
                    "fsdp",
                    sides[step],
                )
                for step in range(middle - 1)
            ]
        )
    total = small_merge(first_small, sides, total, merge_rows)
    small_sum[1] = total
    first_small += len(sides)
    small_stage(first_small, "fsdp", lines, small_sum.at[1])

    line_copies = []
    for index in range(count):
        for copy in side_copies[index]:
            copy.wait_recv()

        def add_side(n, carry, index=index):
            value = sum_core[index][n, side].astype(WIDE)
            for step in range(middle - 1):
                value = value + from_side[index][step, n].astype(WIDE)
            sum_side[index][n] = value.astype(LOW)
            return carry

        lax.fori_loop(0, outer, add_side, 0)
        line_copies.append(
            [
                send(
                    sum_side[index].at[line_steps[step]],
                    from_line[index].at[step],
                    line_sem.at[index, step],
                    "fsdp",
                    lines[step],
                )
                for step in range(outer - 1)
            ]
        )
    total = small_merge(first_small, lines, total, merge_rows)
    small_sum[2] = total
    first_small += len(lines)
    small_stage(first_small, "tp", ranks, small_sum.at[2])

    rank_copies = []
    for index in range(count):
        value = sum_side[index][line].astype(WIDE)
        for step in range(outer - 1):
            line_copies[index][step].wait_recv()
            value = value + from_line[index][step].astype(WIDE)
        wide[index][...] = value
        if 0 < index < tp:
            to_rank[index - 1] = value.astype(LOW)
            rank_copies.append(
                send(
                    to_rank.at[index - 1],
                    from_rank.at[index - 1],
                    rank_sem.at[index - 1],
                    "tp",
                    ranks[index - 1],
                )
            )
    value = wide[0][...]
    for index, copy in enumerate(rank_copies):
        copy.wait_recv()
        value = value + from_rank[index].astype(WIDE)
    outs[0][...] = value
    for index in range(tp, count):
        outs[index - tp + 1][...] = wide[index][...]
    small_out[...] = small_merge(
        first_small,
        ranks,
        total,
        lambda left, right: jnp.where(
            lax.broadcasted_iota(jnp.int32, left.shape, 0) < 4, left + right, left
        ),
    )
    for copies in (*core_copies, *side_copies, *line_copies, rank_copies, small_copies):
        for copy in copies:
            copy.wait_send()


def scatter_end(parts, small, fsdp):
    tp = lax.axis_size("tp")
    outer, middle, inner = split_place(fsdp)
    count = len(parts)
    rows = parts[0].shape[0] // fsdp
    width = parts[0].shape[1]
    shaped = [part.reshape(outer * middle, inner, rows, width) for part in parts]
    in_vmem = pl.BlockSpec(memory_space=pltpu.VMEM)
    peers = (inner - 1) + (middle - 1) + (outer - 1) + (tp - 1)

    def per_part(*shape, dtype=LOW):
        return [pltpu.VMEM((*shape, rows, width), dtype)] * count

    dma = pltpu.SemaphoreType.DMA
    results = count - (tp - 1)
    return pl.pallas_call(
        functools.partial(scatter_kernel, fsdp, tp, count),
        out_shape=(
            *[jax.ShapeDtypeStruct((rows, width), WIDE)] * results,
            jax.ShapeDtypeStruct(small.shape, WIDE),
        ),
        in_specs=[in_vmem] * (count + 1),
        out_specs=[in_vmem] * (results + 1),
        scratch_shapes=[
            *per_part(inner - 1, outer * middle),
            *per_part(outer, middle),
            *per_part(middle - 1, outer),
            *per_part(outer),
            *per_part(outer - 1),
            *per_part(dtype=WIDE),
            pltpu.VMEM((tp - 1, rows, width), LOW),
            pltpu.VMEM((tp - 1, rows, width), LOW),
            pltpu.VMEM((3, *small.shape), WIDE),
            pltpu.VMEM((peers, *small.shape), WIDE),
            dma((count, inner - 1, 2)),
            dma((count, middle - 1, 2)),
            dma((count, outer - 1, 2)),
            dma((tp - 1, 2)),
            dma((peers, 2)),
        ],
        compiler_params=pltpu.CompilerParams(
            collective_id=1, has_side_effects=True, vmem_limit_bytes=VMEM_BYTES
        ),
        name="scatter_end",
        cost_estimate=pl.CostEstimate(
            flops=0, transcendentals=0, bytes_accessed=2 * count * fsdp * rows * width
        ),
    )(*shaped, small)


def up_kernel(chunk, x_ref, w_ref, act_ref, slope_ref):
    for first in range(0, x_ref.shape[0], chunk):
        rows = slice(first, first + chunk)
        pre = jnp.dot(x_ref[rows, :], w_ref[...], preferred_element_type=WIDE)
        scaled = pre * (2**-0.5)
        share = 0.5 + 0.5 * lax.erf(scaled)
        bell = jnp.exp2(scaled * scaled * -math.log2(math.e) - 0.5 * math.log2(2 * math.pi))
        act_ref[rows, :] = (pre * share).astype(LOW)
        slope_ref[rows, :] = (share + pre * bell).astype(LOW)


def block_of(size, wanted):
    return wanted if size % wanted == 0 else size


def up_and_gelu(x, weights, units):
    rows, depth = x.shape
    block = block_of(units, 512)
    shape = jax.ShapeDtypeStruct((rows, units), LOW)
    return pl.pallas_call(
        functools.partial(up_kernel, block_of(rows, 256)),
        out_shape=(shape, shape),
        grid=(units // block,),
        in_specs=[
            whole_block((rows, depth)),
            pl.BlockSpec((depth, block), lambda j: (0, j)),
        ],
        out_specs=[pl.BlockSpec((rows, block), lambda j: (0, j))] * 2,
        compiler_params=pltpu.CompilerParams(vmem_limit_bytes=VMEM_BYTES),
        name="up_and_gelu",
        cost_estimate=pl.CostEstimate(
            flops=3 * rows * depth * units,
            transcendentals=2 * rows * units,
            bytes_accessed=2 * (rows * depth + depth * units + 2 * rows * units),
        ),
    )(x, weights)


def weight_kernel(steps, left_a, right_a, left_b, right_b, out_ref, turned):
    step = pl.program_id(0)

    @pl.when(step == 0)
    def _():
        turned[...] = left_a[...].T

    @pl.when(step == steps)
    def _():
        turned[...] = left_b[...].T

    @pl.when(step < steps)
    def _():
        out_ref[...] = jnp.dot(
            turned[...], right_a[...], preferred_element_type=WIDE
        ).astype(LOW)

    @pl.when(step >= steps)
    def _():
        out_ref[...] = jnp.dot(
            turned[...], right_b[...], preferred_element_type=WIDE
        ).astype(LOW)


def two_weight_grads(left_a, right_a, left_b, right_b):
    rows, depth = left_a.shape
    units = right_a.shape[1]
    block = block_of(units, 512)
    steps = units // block
    return pl.pallas_call(
        functools.partial(weight_kernel, steps),
        out_shape=jax.ShapeDtypeStruct((depth, 2 * units), LOW),
        grid=(2 * steps,),
        in_specs=[
            whole_block((rows, depth)),
            pl.BlockSpec((rows, block), lambda j: (0, jnp.minimum(j, steps - 1))),
            whole_block((rows, depth)),
            pl.BlockSpec((rows, block), lambda j: (0, jnp.maximum(j - steps, 0))),
        ],
        out_specs=pl.BlockSpec((depth, block), lambda j: (0, j)),
        scratch_shapes=[pltpu.VMEM((depth, rows), LOW)],
        compiler_params=pltpu.CompilerParams(vmem_limit_bytes=VMEM_BYTES),
        name="two_weight_grads",
        cost_estimate=pl.CostEstimate(
            flops=6 * rows * depth * units,
            transcendentals=0,
            bytes_accessed=4 * (rows * depth + depth * units + rows * units),
        ),
    )(left_a, right_a, left_b, right_b)


def norm_parts(rows):
    mean = jnp.mean(rows, axis=-1, keepdims=True)
    centered = rows - mean
    inverse = lax.rsqrt(jnp.mean(centered * centered, axis=-1, keepdims=True) + NORM_EPSILON)
    return centered * inverse, inverse


def norm_backward(grad_rows, unit_rows, inverse, gain_row):
    scaled = grad_rows * gain_row
    inner = jnp.mean(scaled * unit_rows, axis=-1, keepdims=True)
    centered = scaled - jnp.mean(scaled, axis=-1, keepdims=True) - unit_rows * inner
    return (
        inverse * centered,
        jnp.sum(grad_rows * unit_rows, axis=0),
        jnp.sum(grad_rows, axis=0),
    )


def dot(left, right, left_dim=1, right_dim=0):
    return lax.dot_general(
        left, right, (((left_dim,), (right_dim,)), ((), ())), preferred_element_type=WIDE
    )


def after(value, *others):
    return lax.optimization_barrier((value, others))[0]


def head_groups(heads):
    if heads >= 8:
        return [heads // 4, heads - heads // 4 - (heads * 3) // 8, (heads * 3) // 8]
    return [1] * heads


def on_device(
    frames,
    cotangent,
    w_query,
    w_key,
    w_value,
    w_output,
    w_up,
    w_down,
    norm_gains,
    norm_biases,
    clip_lengths,
    clip_slot,
):
    fsdp = lax.axis_size("fsdp")
    tp = lax.axis_size("tp")
    me = lax.axis_index("tp")
    own = frames.shape[1]
    padded = own * tp
    cols = w_query.shape[1]
    heads = cols // HEAD_DIM
    units = w_up.shape[1]

    def shift(value, distance):
        pairs = [((i + distance) % tp, i) for i in range(tp)]
        return lax.ppermute(value, "tp", pairs)

    def exchange(pieces):
        return [shift(pieces[s], tp - s) for s in range(1, tp)]

    def columns_of(value, j):
        return value[:, j * own : (j + 1) * own]

    def gather(value):
        return lax.all_gather(value, "fsdp", axis=0, tiled=True)

    def scatter(value):
        return lax.psum_scatter(value, "fsdp", scatter_dimension=0, tiled=True).astype(WIDE)

    own_frames = frames[0]
    cotan = cotangent[0]
    slot = lax.axis_index("fsdp")
    length = jnp.sum(jnp.where(clip_slot == slot, clip_lengths, 0))
    info = jnp.stack([length, me * own, jnp.int32(padded)]).astype(jnp.int32)

    shard_qkv = jnp.concatenate([w_query, w_key, w_value], axis=1)
    shard_rest = jnp.concatenate([w_up, w_down.T], axis=1)
    qkv_blocks, out_blocks, other_frames = gather_start(shard_qkv, w_output.T, own_frames, fsdp)
    w_rest = gather(after(shard_rest, other_frames))
    full_up = w_rest[:, :units]
    down_t = w_rest[:, units:]
    w_qkv = qkv_blocks.reshape(-1, 3 * cols)
    out_pieces = [out_blocks[j].reshape(-1, cols) for j in range(tp)]
    other_frames = [other_frames[s] for s in range(tp - 1)]

    frame_pieces = [own_frames, *other_frames]
    normed_pieces = []
    for piece in frame_pieces:
        unit, _ = norm_parts(piece.astype(WIDE))
        normed_pieces.append((unit * norm_gains[0] + norm_biases[0]).astype(LOW))
    early = own // 2
    cotan_now = after(cotan[:early], other_frames)
    early_cotans = [shift(cotan_now, s) for s in range(1, tp)]
    qkv_pieces = [dot(w_qkv, piece, 0, 1).astype(LOW) for piece in normed_pieces]
    attended_groups = []
    received_groups = []
    totals = []
    tops = []
    first_head = 0
    for count in head_groups(heads):
        if attended_groups:
            info = after(info, attended_groups[-1])
        group_out, group_totals, group_tops = attention_forward(qkv_pieces, info, first_head, count)
        received = []
        for s in range(1, tp):
            other = shift(group_out, s)
            received.append([columns_of(other, (j - s) % tp) for j in range(tp)])
        attended_groups.append(group_out)
        received_groups.append(received)
        totals.append(group_totals)
        tops.append(group_tops)
        first_head += count
    cotan_now = after(cotan[early:], received_groups)
    late_cotans = [shift(cotan_now, s) for s in range(1, tp)]
    attended_own = jnp.concatenate(attended_groups, axis=0)
    attended_rows = [[columns_of(attended_own, j) for j in range(tp)]]
    for s in range(1, tp):
        attended_rows.append(
            [
                jnp.concatenate([received[s - 1][j] for received in received_groups], axis=0)
                for j in range(tp)
            ]
        )
    hidden_pieces = []
    for j in range(tp):
        branch = frame_pieces[j].astype(WIDE)
        for s in range(tp):
            branch = branch + dot(attended_rows[s][j], out_pieces[s], 0, 1)
        hidden_pieces.append(branch)
    normed_two_pieces = []
    for piece in hidden_pieces:
        unit, _ = norm_parts(piece)
        normed_two_pieces.append((unit * norm_gains[1] + norm_biases[1]).astype(LOW))
    normed_two = jnp.concatenate(normed_two_pieces, axis=0)
    hidden_own = hidden_pieces[0]
    activated, slope = up_and_gelu(normed_two, w_rest, units)

    other_cotans = [piece for pair in zip(early_cotans, late_cotans) for piece in pair]
    cotan_all = jnp.concatenate([cotan, *other_cotans], axis=0)
    grad_pre = (dot(cotan_all, down_t) * slope.astype(WIDE)).astype(LOW)

    def rows_of(value, j):
        return value[j * own : (j + 1) * own]

    sent_two = [None] + [
        dot(rows_of(grad_pre, j), full_up, 1, 1).astype(LOW) for j in range(1, tp)
    ]
    received_two = exchange(sent_two)
    gate = after(grad_pre, sent_two[1:])
    total_rest = two_weight_grads(normed_two, gate, cotan_all, activated)
    rest_sum = scatter(total_rest)
    own_two = dot(rows_of(after(gate, total_rest), 0), full_up, 1, 1)
    received_two = [after(item, own_two) for item in received_two]
    grad_normed_two = own_two
    for item in received_two:
        grad_normed_two = grad_normed_two + item.astype(WIDE)
    unit_two, inverse_two = norm_parts(hidden_own)
    grad_from_two, gain_two, bias_two = norm_backward(
        grad_normed_two, unit_two, inverse_two, norm_gains[1]
    )
    grad_hidden = cotan.astype(WIDE) + grad_from_two
    grad_branch = grad_hidden.astype(LOW)

    grad_att = [None] + [
        dot(out_pieces[j], grad_branch, 0, 1).astype(LOW) for j in range(1, tp)
    ]
    received_att = exchange(grad_att)
    grad_branch = after(grad_branch, grad_att[1:])
    late_act = after(activated, grad_att[1:])
    sent_mlp = [dot(rows_of(late_act, j), down_t, 1, 1) for j in range(tp)]
    grad_att_own = dot(out_pieces[0], grad_branch, 0, 1).astype(LOW)
    total_out = [dot(grad_branch, attended_rows[s][0], 0, 1).astype(LOW) for s in range(tp)]
    received_att = [after(item, total_out, grad_att_own, sent_mlp) for item in received_att]
    late_mlp = [None] + [after(piece.astype(LOW), received_att) for piece in sent_mlp[1:]]
    received_mlp = exchange(late_mlp)
    grad_att_pieces = [grad_att_own, *received_att[::-1]]
    normed_all = jnp.concatenate(normed_pieces, axis=0)
    all_totals = jnp.concatenate(totals, axis=0)
    grad_qkv = attention_backward(qkv_pieces, attended_own, grad_att_pieces, all_totals, info, 0)
    sent_one = [None] + [
        dot(columns_of(grad_qkv, j), w_qkv, 0, 1).astype(LOW) for j in range(1, tp)
    ]
    received_one = exchange(sent_one)
    gate = after(grad_qkv, sent_one[1:])
    total_qkv = [
        dot(normed_all, gate[n * cols : (n + 1) * cols], 0, 1).astype(LOW) for n in range(3)
    ]
    own_one = dot(columns_of(gate, 0), w_qkv, 0, 1)
    frames_late = [after(piece, grad_qkv) for piece in frame_pieces]
    units_one = [norm_parts(piece.astype(WIDE)) for piece in frames_late]
    gain_one = jnp.sum(own_one * units_one[0][0], axis=0)
    bias_one = jnp.sum(own_one, axis=0)
    for j in range(1, tp):
        part = sent_one[j].astype(WIDE)
        gain_one = gain_one + jnp.sum(part * units_one[j][0], axis=0)
        bias_one = bias_one + jnp.sum(part, axis=0)

    head_top = jnp.concatenate(tops, axis=0)[:, 0] * SCORE_SCALE
    head_row = jnp.pad(head_top, (0, gain_one.shape[0] - heads))
    blank = jnp.zeros_like(head_row)
    small = jnp.stack([gain_one, gain_two, bias_one, bias_two, head_row, blank, blank, blank])
    out_sum, query_sum, key_sum, value_sum, small = scatter_end(
        [*total_out, *total_qkv], small, fsdp
    )
    head_top = small[4, :heads]
    received_one = [after(item, small) for item in received_one]
    grad_normed_one = own_one
    for item in received_one:
        grad_normed_one = grad_normed_one + item.astype(WIDE)
    grad_from_one, _, _ = norm_backward(grad_normed_one, *units_one[0], norm_gains[0])
    grad_frames = grad_hidden + grad_from_one
    output = hidden_own + sent_mlp[0]
    for item in received_mlp:
        output = output + item.astype(WIDE)

    factor = jnp.sqrt(CLIP_LIMIT / jnp.maximum(head_top, CLIP_LIMIT))
    columns = jnp.repeat(factor, HEAD_DIM)
    return (
        output.astype(LOW)[None],
        grad_frames[None],
        query_sum,
        key_sum,
        value_sum,
        out_sum.T,
        rest_sum[:, :units],
        rest_sum[:, units:].T,
        small[0:2],
        small[2:4],
        w_query.astype(WIDE) * columns[None, :],
        w_key.astype(WIDE) * columns[None, :],
    )


def solution(mesh):
    rows = P("fsdp", "tp", None)
    wide = P("fsdp", "tp")
    tall = P("tp", "fsdp")
    none = P()
    return jax.shard_map(
        on_device,
        mesh=mesh,
        in_specs=(rows, rows, wide, wide, wide, tall, wide, tall, none, none, none, none),
        out_specs=(rows, rows, wide, wide, wide, tall, wide, tall, none, none, wide, wide),
        check_vma=False,
    )
```

profile of v0, /device:TPU:0, one launch (start us, length us, event | category | flops | bytes accessed | tf_op | source)
XLA Modules:
  0.0 507.5 jit_solution(18105399069818657645)
XLA Ops:
  7.3 2.2 pad_maximum_fusion.7
  9.5 1.7 pad_maximum_fusion.10.shard_qkv
  11.2 60.2 %gather_start.1 = (bf16[16,80,1920]{2,1,0:T(8,128)(2,1)}, bf16[2,16,80,640]{3,2,1,0:T(8,128)(2,1)}, bf16[1,768,1280]{2,1,0:T(8,128)(2,1)}) custom-call(bf16[80,1920]{1,0:T(8,128)(2,1)} %pad_maximum_fusion.10.shard_qkv, bf16[80,640]{1,0:T(8,128)(2,1)} %bitcast.83, bf16[768,1280]{1,0:T(8,128)(2,1)} %bitcast.59), custom_call_target="tpu_custom_call" | custom-call | bytes 6553600 | tf_op jit(solution)/shard_map/gather_start/pallas_call | solution.py:331
  72.2 1.2 pad_add_fusion.info_ref
  73.5 2.0 convert_reduce_fusion
  77.3 6.9 %convolution_convert_fusion.1.refs_1_.refs_3_.refs_5_ = bf16[1920,768]{1,0:T(8,128)(2,1)} fusion(bf16[1280,1920]{1,0:T(8,128)(2,1)S(1)} %bitcast.88, bf16[1,768,1280]{2,1,0:T(8,128)(2,1)S(1)} %copy-done.5, f32[768]{0:T(1024)S(1)} %add_rsqrt_fusion.4, f32[768]{0:T(1024)S(1)} %broadcast_multiply_fusion.8, f32[1280]{0:T(1024)S(1)} %get-tuple-element.95, ...), kind=kOutput, calls=%fused_computation.75 | convolution fusion | flops 3782246400 | bytes 9846784 | tf_op jit(solution)/shard_map/dot_general | solution.py:710
  84.2 6.3 %convolution_convert_fusion.2.refs_0_.refs_2_.refs_4_ = bf16[1920,768]{1,0:T(8,128)(2,1)} fusion(bf16[1280,1920]{1,0:T(8,128)(2,1)S(1)} %bitcast.89, bf16[1,768,1280]{2,1,0:T(8,128)(2,1)S(1)} %copy-done.3, f32[1280]{0:T(1024)S(1)} %get-tuple-element.95, f32[1280]{0:T(1024)S(1)} %get-tuple-element.93, f32[768]{0:T(1024)S(1)} %add_rsqrt_fusion.5, ...), kind=kOutput, calls=%fused_computation.76 | convolution fusion | flops 3782246400 | bytes 9846784 | tf_op jit(solution)/shard_map/dot_general | solution.py:710
  90.5 9.1 %attention_forward.3 = (bf16[160,1536]{1,0:T(8,128)(2,1)}, f32[2,1536]{1,0:T(2,128)}, f32[2,128]{1,0:T(2,128)}) custom-call(s32[3]{0:T(128)} %pad_add_fusion.info_ref, bf16[1920,768]{1,0:T(8,128)(2,1)} %convolution_convert_fusion.2.refs_0_.refs_2_.refs_4_, bf16[1920,768]{1,0:T(8,128)(2,1)} %convolution_convert_fusion.1.refs_1_.refs_3_.refs_5_, ...), custom_call_target="tpu_custom_call" | custom-call | flops 8455716864 | bytes 1966080 | tf_op jit(solution)/shard_map/attention_forward/pallas_call | solution.py:87
  99.6 1.6 collective-permute-start
  101.1 12.2 %attention_forward.4 = (bf16[240,1536]{1,0:T(8,128)(2,1)}, f32[3,1536]{1,0:T(4,128)}, f32[3,128]{1,0:T(4,128)}) custom-call(s32[3]{0:T(128)} %pad_add_fusion.info_ref, bf16[1920,768]{1,0:T(8,128)(2,1)} %convolution_convert_fusion.2.refs_0_.refs_2_.refs_4_, bf16[1920,768]{1,0:T(8,128)(2,1)} %convolution_convert_fusion.1.refs_1_.refs_3_.refs_5_, ...), custom_call_target="tpu_custom_call" | custom-call | flops 12683575296 | bytes 2949120 | tf_op jit(solution)/shard_map/attention_forward/pallas_call | solution.py:87
  113.8 12.4 %attention_forward.5 = (bf16[240,1536]{1,0:T(8,128)(2,1)}, f32[3,1536]{1,0:T(4,128)}, f32[3,128]{1,0:T(4,128)}) custom-call(s32[3]{0:T(128)} %pad_add_fusion.info_ref, bf16[1920,768]{1,0:T(8,128)(2,1)} %convolution_convert_fusion.2.refs_0_.refs_2_.refs_4_, bf16[1920,768]{1,0:T(8,128)(2,1)} %convolution_convert_fusion.1.refs_1_.refs_3_.refs_5_, ...), custom_call_target="tpu_custom_call" | custom-call | flops 12683575296 | bytes 2949120 | tf_op jit(solution)/shard_map/attention_forward/pallas_call | solution.py:87
  126.2 1.6 collective-permute-start.2
  127.8 1.7 slice_bitcast_fusion.1
  129.5 1.2 collective-permute-start.3
  131.2 2.4 copy-done.6
  133.7 1.7 convert_add_fusion
  135.4 3.1 fusion.27
  138.7 1.7 convert_add_fusion.1
  141.9 6.8 %collective-permute-done.2 = bf16[240,1536]{1,0:T(8,128)(2,1)S(1)} collective-permute-done((bf16[240,1536]{1,0:T(8,128)(2,1)}, bf16[240,1536]{1,0:T(8,128)(2,1)S(1)}, u32[]{:S(2)}, u32[]{:S(2)}) %collective-permute-start.2) | collective-permute-done | bytes 737312 | tf_op jit(solution)/shard_map/ppermute | solution.py:750
  148.8 1.1 fusion.85
  150.4 1.9 fusion.90
  152.9 1.9 fusion.89
  155.3 1.5 add_convert_fusion.2
  156.8 2.2 pad_maximum_fusion.x_ref.left_a
  159.0 10.8 %collective-permute-done.3 = bf16[384,1280]{1,0:T(8,128)(2,1)S(1)} collective-permute-done((bf16[384,1280]{1,0:T(8,128)(2,1)S(1)}, bf16[384,1280]{1,0:T(8,128)(2,1)S(1)}, u32[]{:S(2)}, u32[]{:S(2)}) %collective-permute-start.3) | collective-permute-done | bytes 983072 | tf_op jit(solution)/shard_map/ppermute | solution.py:750
  169.8 20.2 %collective-permute-done.4 = bf16[384,1280]{1,0:T(8,128)(2,1)S(1)} collective-permute-done((bf16[384,1280]{1,0:T(8,128)(2,1)S(1)}, bf16[384,1280]{1,0:T(8,128)(2,1)S(1)}, u32[]{:S(2)}, u32[]{:S(2)}) %collective-permute-start.4) | collective-permute-done | bytes 983072 | tf_op jit(solution)/shard_map/ppermute | solution.py:750
  190.0 0.9 copy-done.22
  190.9 2.2 pad_maximum_fusion.1.left_b
  193.1 18.4 %up_and_gelu.1 = (bf16[1536,2560]{1,0:T(8,128)(2,1)}, bf16[1536,2560]{1,0:T(8,128)(2,1)}) custom-call(bf16[1536,1280]{1,0:T(8,128)(2,1)} %pad_maximum_fusion.x_ref.left_a, bf16[1280,5120]{1,0:T(8,128)(2,1)} %all-gather.2.cloned.1.call-done.w_ref), custom_call_target="tpu_custom_call" | custom-call | flops 15099494400 | bytes 26214400 | tf_op jit(solution)/shard_map/up_and_gelu/pallas_call | solution.py:621
  211.5 17.7 %multiply_convert_fusion.right_a = bf16[1536,2560]{1,0:T(8,128)(2,1)} fusion(bf16[1536,2560]{1,0:T(8,128)(2,1)} %get-tuple-element.59, bf16[1280,5120]{1,0:T(8,128)(2,1)} %all-gather.2.cloned.1.call-done.w_ref, bf16[384,1280]{1,0:T(8,128)(2,1)} %copy-done.22, bf16[384,1280]{1,0:T(8,128)(2,1)} %copy-done.21, bf16[768,1280]{1,0:T(8,128)(2,1)S(1)} %bitcast.69), kind=kOutput, calls=%fused_computation | convolution fusion | flops 10089922560 | bytes 26214400 | tf_op jit(solution)/shard_map/dot_general | solution.py:710
  229.2 9.9 %fusion.41 = bf16[768,1280]{1,0:T(8,128)(2,1)} fusion(bf16[1280,5120]{1,0:T(8,128)(2,1)} %all-gather.2.cloned.1.call-done.w_ref, bf16[1536,2560]{1,0:T(8,128)(2,1)} %multiply_convert_fusion.right_a), kind=kOutput, calls=%fused_computation.73 | convolution fusion | flops 5034147840 | bytes 12451840 | tf_op jit(solution)/shard_map/dot_general | solution.py:710
  239.5 30.1 %two_weight_grads.1 = bf16[1280,5120]{1,0:T(8,128)(2,1)} custom-call(bf16[1536,1280]{1,0:T(8,128)(2,1)} %pad_maximum_fusion.x_ref.left_a, bf16[1536,2560]{1,0:T(8,128)(2,1)} %multiply_convert_fusion.right_a, bf16[1536,1280]{1,0:T(8,128)(2,1)} %pad_maximum_fusion.1.left_b, bf16[1536,2560]{1,0:T(8,128)(2,1)} %get-tuple-element.63.right_b), custom_call_target="tpu_custom_call" | custom-call | flops 30198988800 | bytes 36700160 | tf_op jit(solution)/shard_map/two_weight_grads/pallas_call | solution.py:669
  269.6 9.5 %fusion = f32[768,1280]{1,0:T(8,128)S(1)} fusion(bf16[1280,5120]{1,0:T(8,128)(2,1)} %all-gather.2.cloned.1.call-done.w_ref, bf16[1536,2560]{1,0:T(8,128)(2,1)} %multiply_convert_fusion.right_a), kind=kOutput, calls=%fused_computation.7 | convolution fusion | flops 5033164800 | bytes 14417920 | tf_op jit(solution)/shard_map/dot_general | solution.py:710
  279.0 4.3 collective-permute-done.5
  283.4 3.5 multiply_reduce_fusion
  286.9 4.6 fusion.83
  291.4 1.5 convolution_convert_fusion.9
  293.3 2.9 convolution_convert_fusion.3
  296.2 2.9 convolution_convert_fusion.4
  299.4 2.5 convolution_convert_fusion.8.refs_6_
  301.8 1.2 slice-done.2
  303.0 1.5 slice-done.7
  304.7 7.2 %fusion.6 = f32[768,1280]{1,0:T(8,128)} fusion(bf16[1280,5120]{1,0:T(8,128)(2,1)S(1)} %bitcast.85, bf16[1536,2560]{1,0:T(8,128)(2,1)S(1)} %bitcast.98), kind=kOutput, calls=%fused_computation.13 | convolution fusion | flops 5033164800 | bytes 14417920 | tf_op jit(solution)/shard_map/dot_general | solution.py:710
  311.9 6.6 %fusion.4 = bf16[768,1280]{1,0:T(8,128)(2,1)} fusion(bf16[1280,5120]{1,0:T(8,128)(2,1)S(1)} %bitcast.85, bf16[1536,2560]{1,0:T(8,128)(2,1)S(1)} %bitcast.98), kind=kOutput, calls=%fused_computation.11 | convolution fusion | flops 5033164800 | bytes 12451840 | tf_op jit(solution)/shard_map/dot_general | solution.py:710
  318.5 51.4 %attention_backward.1 = bf16[3,640,1536]{2,1,0:T(8,128)(2,1)} custom-call(s32[3]{0:T(128)} %pad_add_fusion.info_ref, bf16[1920,768]{1,0:T(8,128)(2,1)} %convolution_convert_fusion.2.refs_0_.refs_2_.refs_4_, bf16[1920,768]{1,0:T(8,128)(2,1)} %convolution_convert_fusion.1.refs_1_.refs_3_.refs_5_, ...), custom_call_target="tpu_custom_call" | custom-call | flops 62813896704 | bytes 15728640 | tf_op jit(solution)/shard_map/attention_backward/pallas_call | solution.py:168
  371.4 9.7 %convert_reduce_fusion.3 = (f32[1280]{0:T(1024)S(1)}, f32[1280]{0:T(1024)S(1)}, bf16[768,1280]{1,0:T(8,128)(2,1)}) fusion(f32[768]{0:T(1024)S(1)} %add_rsqrt_fusion, f32[768]{0:T(1024)S(1)} %broadcast_multiply_fusion.2, bf16[768,1280]{1,0:T(8,128)(2,1)S(1)} %bitcast.67, bf16[1280,1920]{1,0:T(8,128)(2,1)} %bitcast.86, bf16[1920,1536]{1,0:T(8,128)(2,1)} %bitcast.90), kind=kOutput, calls=%fused_computation.18 | convolution fusion | flops 3782735360 | bytes 11812864 | tf_op jit(solution)/shard_map/dot_general | solution.py:710
  381.1 1.8 collective-permute-start.8
  384.2 4.6 convolution_convert_fusion.5
  388.8 8.9 %fusion.82 = (f32[1280]{0:T(1024)S(1)}, f32[1280]{0:T(1024)S(1)}, f32[768,1280]{1,0:T(8,128)}) fusion(f32[768]{0:T(1024)S(1)} %add_rsqrt_fusion.1, f32[768]{0:T(1024)S(1)} %broadcast_multiply_fusion.3, bf16[768,1280]{1,0:T(8,128)(2,1)S(1)} %bitcast.62, bf16[1280,1920]{1,0:T(8,128)(2,1)} %bitcast.87, bf16[1920,1536]{1,0:T(8,128)(2,1)S(1)} %bitcast.94), kind=kOutput, calls=%fused_computation.155 | convolution fusion | flops 3780769280 | bytes 13780992 | tf_op jit(solution)/shard_map/dot_general | solution.py:710
  397.7 4.4 convolution_convert_fusion.6
  402.1 4.4 convolution_convert_fusion.7
  407.3 70.8 %scatter_end.1 = (f32[80,640]{1,0:T(8,128)}, f32[80,640]{1,0:T(8,128)}, f32[80,640]{1,0:T(8,128)}, f32[80,640]{1,0:T(8,128)}, f32[8,1280]{1,0:T(8,128)}) custom-call(bf16[8,2,80,640]{3,2,1,0:T(8,128)(2,1)} %bitcast.77, bf16[8,2,80,640]{3,2,1,0:T(8,128)(2,1)} %bitcast.76, bf16[8,2,80,640]{3,2,1,0:T(8,128)(2,1)} %bitcast.80, bf16[8,2,80,640]{3,2,1,0:T(8,128)(2,1)} %bitcast.79, ...), custom_call_target="tpu_custom_call" | custom-call | bytes 8192000 | tf_op jit(solution)/shard_map/scatter_end/pallas_call | solution.py:567
  478.1 0.7 sqrt_bitcast_fusion
  478.9 0.8 convert_multiply_fusion.1
  479.7 1.5 fusion.88
  481.2 4.2 fusion.65
  485.5 0.7 copy-done.14
  486.2 4.0 fusion.53
  490.2 4.2 fusion.34
  494.5 1.4 convert_element_type.151
  495.9 0.9 slice_bitcast_fusion.2
  496.8 1.0 slice.158
  497.8 0.7 copy.30
  498.5 0.7 copy.31
  (177 shorter events, 12.6 us)
Async XLA Ops:
  7.2 68.4 %copy-start.3 = (bf16[1,768,1280]{2,1,0:T(8,128)(2,1)S(1)}, bf16[1,768,1280]{2,1,0:T(8,128)(2,1)}, u32[]{:S(2)}) copy-start(bf16[1,768,1280]{2,1,0:T(8,128)(2,1)} %param.12) | copy-start | bytes 5898244
  7.2 64.3 %copy-start.45 = (s32[16]{0:T(128)S(1)}, s32[16]{0:T(128)}, u32[]{:S(2)}) copy-start(s32[16]{0:T(128)} %param.22) | copy-start | bytes 196
  7.2 64.3 %copy-start.46 = (s32[16]{0:T(128)S(1)}, s32[16]{0:T(128)}, u32[]{:S(2)}) copy-start(s32[16]{0:T(128)} %param.23) | copy-start | bytes 196
  7.2 66.2 %copy-start.40 = (f32[2,1280]{1,0:T(2,128)S(1)}, f32[2,1280]{1,0:T(2,128)}, u32[]{:S(2)}) copy-start(f32[2,1280]{1,0:T(2,128)} %param.20) | copy-start | bytes 30724
  7.2 66.2 %copy-start.41 = (f32[2,1280]{1,0:T(2,128)S(1)}, f32[2,1280]{1,0:T(2,128)}, u32[]{:S(2)}) copy-start(f32[2,1280]{1,0:T(2,128)} %param.21) | copy-start | bytes 30724
  7.2 185.9 %all-gather.2.cloned.1.call-start = ((), (), s32[]{:S(2)}) async-start(), calls=%async_computation.1 | async-start | bytes 13926400 | tf_op jit(solution)/shard_map/all_gather | solution.py:759
  71.5 423.0 %reduce-scatter.2.cloned.1.call-start = ((), (), s32[]{:S(2)}) async-start(), calls=%async_computation.2 | async-start | bytes 13926400 | tf_op jit(solution)/shard_map/reduce_scatter | solution.py:762
  71.6 4.4 copy-start.5
  73.5 61.9 %copy-start.32 = (f32[1280]{0:T(1024)}, f32[1280]{0:T(1024)S(1)}, u32[]{:S(2)}) copy-start(f32[1280]{0:T(1024)S(1)} %get-tuple-element.93) | copy-start | bytes 15364
  73.5 3.7 copy-start.47
  99.6 42.3 %collective-permute-start = (bf16[160,1536]{1,0:T(8,128)(2,1)}, bf16[160,1536]{1,0:T(8,128)(2,1)S(1)}, u32[]{:S(2)}, u32[]{:S(2)}) collective-permute-start(bf16[160,1536]{1,0:T(8,128)(2,1)} %get-tuple-element.49), channel_id=1, source_target_pairs={{1,0},{0,1},{3,2},{2,3},{5,4},{4,5},{7,6},{6,7},{9,8},{8,9},{11,10... | collective-permute-start | bytes 1474568 | tf_op jit(solution)/shard_map/ppermute | solution.py:750
  113.3 35.4 %collective-permute-start.1 = (bf16[240,1536]{1,0:T(8,128)(2,1)}, bf16[240,1536]{1,0:T(8,128)(2,1)}, u32[]{:S(2)}, u32[]{:S(2)}) collective-permute-start(bf16[240,1536]{1,0:T(8,128)(2,1)} %get-tuple-element.51), channel_id=1, source_target_pairs={{1,0},{0,1},{3,2},{2,3},{5,4},{4,5},{7,6},{6,7},{9,8},{8,9},{11,10... | collective-permute-start | bytes 2211848 | tf_op jit(solution)/shard_map/ppermute | solution.py:750
  126.1 4.6 copy-start.25
  126.1 4.6 copy-start.23
  126.2 4.7 copy-start.24
  126.2 4.7 copy-start.15
  126.2 22.5 %collective-permute-start.2 = (bf16[240,1536]{1,0:T(8,128)(2,1)}, bf16[240,1536]{1,0:T(8,128)(2,1)S(1)}, u32[]{:S(2)}, u32[]{:S(2)}) collective-permute-start(bf16[240,1536]{1,0:T(8,128)(2,1)} %get-tuple-element.53), channel_id=1, source_target_pairs={{1,0},{0,1},{3,2},{2,3},{5,4},{4,5},{7,6},{6,7},{9,8},{8,9},{11,10... | collective-permute-start | bytes 2211848 | tf_op jit(solution)/shard_map/ppermute | solution.py:750
  129.5 40.2 %collective-permute-start.3 = (bf16[384,1280]{1,0:T(8,128)(2,1)S(1)}, bf16[384,1280]{1,0:T(8,128)(2,1)S(1)}, u32[]{:S(2)}, u32[]{:S(2)}) collective-permute-start(bf16[384,1280]{1,0:T(8,128)(2,1)S(1)} %get-tuple-element.57), channel_id=1, source_target_pairs={{1,0},{0,1},{3,2},{2,3},{5,4},{4,5},{7,6},{6,7},{9,8},{8,9},{11,10... | collective-permute-start | bytes 2949128 | tf_op jit(solution)/shard_map/ppermute | solution.py:750
  130.8 2.8 copy-start.6
  130.9 7.7 %copy-start.34 = (bf16[640,1536]{1,0:T(8,128)(2,1)}, bf16[640,1536]{1,0:T(8,128)(2,1)S(1)}, u32[]{:S(2)}) copy-start(bf16[640,1536]{1,0:T(8,128)(2,1)S(1)} %constant_dynamic-update-slice_fusion.refs_8_) | copy-start | bytes 5898244
  131.2 7.4 %copy-start.19 = (bf16[1,16,80,640]{3,2,1,0:T(8,128)(2,1)}, bf16[1,16,80,640]{3,2,1,0:T(8,128)(2,1)S(1)}, u32[]{:S(2)}) copy-start(bf16[1,16,80,640]{3,2,1,0:T(8,128)(2,1)S(1)} %get-tuple-element.99) | copy-start | bytes 4915204
  131.2 21.6 %copy-start.12 = (bf16[1,16,80,640]{3,2,1,0:T(8,128)(2,1)}, bf16[1,16,80,640]{3,2,1,0:T(8,128)(2,1)S(1)}, u32[]{:S(2)}) copy-start(bf16[1,16,80,640]{3,2,1,0:T(8,128)(2,1)S(1)} %get-tuple-element.98) | copy-start | bytes 4915204
  138.6 1.8 copy-start.42
  138.6 1.8 copy-start.43
  138.6 2.6 copy-start.36
  138.6 2.5 copy-start.37
  138.7 2.5 copy-start.39
  149.9 40.1 %collective-permute-start.4 = (bf16[384,1280]{1,0:T(8,128)(2,1)S(1)}, bf16[384,1280]{1,0:T(8,128)(2,1)S(1)}, u32[]{:S(2)}, u32[]{:S(2)}) collective-permute-start(bf16[384,1280]{1,0:T(8,128)(2,1)S(1)} %get-tuple-element.58), channel_id=1, source_target_pairs={{1,0},{0,1},{3,2},{2,3},{5,4},{4,5},{7,6},{6,7},{9,8},{8,9},{11,10... | collective-permute-start | bytes 2949128 | tf_op jit(solution)/shard_map/ppermute | solution.py:750
  154.7 2.0 copy-start
  156.8 34.2 %copy-start.9 = (bf16[1,768,1280]{2,1,0:T(8,128)(2,1)S(1)}, bf16[1,768,1280]{2,1,0:T(8,128)(2,1)}, u32[]{:S(2)}) copy-start(bf16[1,768,1280]{2,1,0:T(8,128)(2,1)} %param.13) | copy-start | bytes 5898244
  169.8 20.2 %copy-start.21 = (bf16[384,1280]{1,0:T(8,128)(2,1)}, bf16[384,1280]{1,0:T(8,128)(2,1)S(1)}, u32[]{:S(2)}) copy-start(bf16[384,1280]{1,0:T(8,128)(2,1)S(1)} %collective-permute-done.3) | copy-start | bytes 2949124
  239.0 44.3 %collective-permute-start.5 = (bf16[768,1280]{1,0:T(8,128)(2,1)}, bf16[768,1280]{1,0:T(8,128)(2,1)}, u32[]{:S(2)}, u32[]{:S(2)}) collective-permute-start(bf16[768,1280]{1,0:T(8,128)(2,1)} %fusion.41), channel_id=1, source_target_pairs={{1,0},{0,1},{3,2},{2,3},{5,4},{4,5},{7,6},{6,7},{9,8},{8,9},{11,10... | collective-permute-start | bytes 5898248 | tf_op jit(solution)/shard_map/ppermute | solution.py:750
  269.6 13.8 %copy-start.1 = (f32[768,1280]{1,0:T(8,128)S(1)}, f32[768,1280]{1,0:T(8,128)}, u32[]{:S(2)}) copy-start(f32[768,1280]{1,0:T(8,128)} %copy-done) | copy-start | bytes 11796484
  286.8 4.6 copy-start.13
  291.4 10.4 %slice-start.6 = ((s8[7864320]{0:T(1024)(128)(4,1)}), s8[4194304]{0:T(1024)(128)(4,1)S(1)}, s32[]{:S(2)}) async-start(s8[7864320]{0:T(1024)(128)(4,1)} %bitcast.97), calls=%async_computation.9 | async-start | bytes 8388608
  292.9 25.6 %collective-permute-start.6 = (bf16[640,768]{1,0:T(8,128)(2,1)S(1)}, bf16[640,768]{1,0:T(8,128)(2,1)}, u32[]{:S(2)}, u32[]{:S(2)}) collective-permute-start(bf16[640,768]{1,0:T(8,128)(2,1)S(1)} %convolution_convert_fusion.9), channel_id=1, source_target_pairs={{1,0},{0,1},{3,2},{2,3},{5,4},{4,5},{7,6},{6,7},{9,8},{8,9},{11,10... | collective-permute-start | bytes 2949128 | tf_op jit(solution)/shard_map/ppermute | solution.py:750
  293.3 3.0 copy-start.35
  293.3 8.6 %slice-start = ((s8[13107200]{0:T(1024)(128)(4,1)}), s8[4194304]{0:T(1024)(128)(4,1)S(1)}, s32[]{:S(2)}) async-start(s8[13107200]{0:T(1024)(128)(4,1)} %bitcast.84), calls=%async_computation.3 | async-start | bytes 8388608
  293.3 8.6 %slice-start.1 = ((s8[13107200]{0:T(1024)(128)(4,1)}), s8[4194304]{0:T(1024)(128)(4,1)S(1)}, s32[]{:S(2)}) async-start(s8[13107200]{0:T(1024)(128)(4,1)} %bitcast.84), calls=%async_computation.4 | async-start | bytes 8388608
  296.2 3.1 copy-start.20
  296.2 6.8 %slice-start.2 = ((s8[13107200]{0:T(1024)(128)(4,1)}), s8[4194304]{0:T(1024)(128)(4,1)S(1)}, s32[]{:S(2)}) async-start(s8[13107200]{0:T(1024)(128)(4,1)} %bitcast.84), calls=%async_computation.5 | async-start | bytes 8388608
  296.2 8.3 %slice-start.7 = ((s8[7864320]{0:T(1024)(128)(4,1)}), s8[3670016]{0:T(1024)(128)(4,1)S(1)}, s32[]{:S(2)}) async-start(s8[7864320]{0:T(1024)(128)(4,1)} %bitcast.97), calls=%async_computation.10 | async-start | bytes 7340032
  299.4 5.3 %slice-start.3 = ((s8[13107200]{0:T(1024)(128)(4,1)}), s8[524288]{0:T(1024)(128)(4,1)S(1)}, s32[]{:S(2)}) async-start(s8[13107200]{0:T(1024)(128)(4,1)} %bitcast.84), calls=%async_computation.6 | async-start | bytes 1048576
  318.5 51.4 %copy-start.7 = (bf16[1,768,1280]{2,1,0:T(8,128)(2,1)S(1)}, bf16[1,768,1280]{2,1,0:T(8,128)(2,1)}, u32[]{:S(2)}) copy-start(bf16[1,768,1280]{2,1,0:T(8,128)(2,1)} %get-tuple-element.48) | copy-start | bytes 5898244
  370.9 13.3 %slice-start.4 = ((s8[5898240]{0:T(1024)(128)(4,1)}), s8[4194304]{0:T(1024)(128)(4,1)S(1)}, s32[]{:S(2)}) async-start(s8[5898240]{0:T(1024)(128)(4,1)} %bitcast.91), calls=%async_computation.7 | async-start | bytes 8388608
  371.4 11.7 %copy-start.4 = (bf16[1,768,1280]{2,1,0:T(8,128)(2,1)S(1)}, bf16[1,768,1280]{2,1,0:T(8,128)(2,1)}, u32[]{:S(2)}) copy-start(bf16[1,768,1280]{2,1,0:T(8,128)(2,1)} %param.12) | copy-start | bytes 5898244
  371.4 12.7 %slice-start.5 = ((s8[5898240]{0:T(1024)(128)(4,1)}), s8[1703936]{0:T(1024)(128)(4,1)S(1)}, s32[]{:S(2)}) async-start(s8[5898240]{0:T(1024)(128)(4,1)} %bitcast.91), calls=%async_computation.8 | async-start | bytes 3407872
  381.1 3.1 copy-start.17
  381.1 3.1 copy-start.18
  381.1 100.0 %collective-permute-start.8 = (bf16[768,1280]{1,0:T(8,128)(2,1)}, bf16[768,1280]{1,0:T(8,128)(2,1)}, u32[]{:S(2)}, u32[]{:S(2)}) collective-permute-start(bf16[768,1280]{1,0:T(8,128)(2,1)} %get-tuple-element.121), channel_id=1, source_target_pairs={{1,0},{0,1},{3,2},{2,3},{5,4},{4,5},{7,6},{6,7},{9,8},{8,9},{11,10... | collective-permute-start | bytes 5898248 | tf_op jit(solution)/shard_map/ppermute | solution.py:750
  383.0 102.5 %collective-permute-start.7 = (bf16[768,1280]{1,0:T(8,128)(2,1)}, bf16[768,1280]{1,0:T(8,128)(2,1)}, u32[]{:S(2)}, u32[]{:S(2)}) collective-permute-start(bf16[768,1280]{1,0:T(8,128)(2,1)} %fusion.4), channel_id=1, source_target_pairs={{1,0},{0,1},{3,2},{2,3},{5,4},{4,5},{7,6},{6,7},{9,8},{8,9},{11,10... | collective-permute-start | bytes 5898248 | tf_op jit(solution)/shard_map/ppermute | solution.py:750
  402.1 4.5 copy-start.38
  407.3 71.6 %copy-start.26 = (bf16[80,640]{1,0:T(8,128)(2,1)S(1)}, bf16[80,640]{1,0:T(8,128)(2,1)}, u32[]{:S(2)}) copy-start(bf16[80,640]{1,0:T(8,128)(2,1)} %param.15) | copy-start | bytes 307204
  407.3 71.6 %copy-start.27 = (bf16[80,640]{1,0:T(8,128)(2,1)S(1)}, bf16[80,640]{1,0:T(8,128)(2,1)}, u32[]{:S(2)}) copy-start(bf16[80,640]{1,0:T(8,128)(2,1)} %param.14) | copy-start | bytes 307204
  407.3 73.9 %copy-start.33 = (f32[1280]{0:T(1024)S(1)}, f32[1280]{0:T(1024)}, u32[]{:S(2)}) copy-start(f32[1280]{0:T(1024)} %copy-done.32) | copy-start | bytes 15364
  481.2 4.3 copy-start.2
  481.2 5.1 copy-start.14
  485.5 4.7 copy-start.10
  485.5 4.7 copy-start.11
  494.4 3.4 copy-start.31
  494.4 4.0 copy-start.30
  494.4 4.7 copy-start.29
  494.4 5.4 %copy-start.28 = (f32[80,640]{1,0:T(8,128)S(1)}, f32[80,640]{1,0:T(8,128)}, u32[]{:S(2)}) copy-start(f32[80,640]{1,0:T(8,128)} %get-tuple-element.81) | copy-start | bytes 614404
  494.5 2.4 copy-start.16
  (3 other events, 4.3 us)
Sparse Core Ops, SparseCore 0:
  71.6 114.0 all-gather.1
  269.7 148.8 reduce-scatter.1
where the time goes:
time: 511 us; the launch traced here: 508 us
  Pallas kernels  264 us (52%)
  matrix products  113 us (22%)
  other arithmetic  45.5 us (9%)
  waiting for transfers between devices  42.2 us (8%)
  local copies, waits for them, and re-layouts  18.9 us (4%)
  between operations  15.1 us (3%)
  starting transfers between devices  8.21 us (2%)
    dot_general x20, matrix products, dot(): lax.dot_general(left, right, (((left_dim,), (right_dim,)), ((), ())), pre...  113 us
    pallas_call x1, Pallas kernels, scatter_end(): pl.pallas_call(functools.partial(scatter_kernel, fsdp, tp, count), out_sh...  70.8 us
    pallas_call x1, Pallas kernels, gather_start(): pl.pallas_call(functools.partial(gather_kernel, fsdp, tp), out_shape=(jax...  60.2 us
    pallas_call x1, Pallas kernels, attention_backward(): pl.pallas_call(functools.partial(backward_kernel, len(pieces)), out_shape...  51.4 us
    ppermute x9, waiting for transfers between devices, shift(): return lax.ppermute(value, 'tp', pairs)  42.2 us
    pallas_call x3, Pallas kernels, attention_forward(): pl.pallas_call(functools.partial(forward_kernel, len(pieces)), out_shape=...  33.7 us
    pallas_call x1, Pallas kernels, two_weight_grads(): pl.pallas_call(functools.partial(weight_kernel, steps), out_shape=jax.Sha...  30.1 us
    pallas_call x1, Pallas kernels, up_and_gelu(): pl.pallas_call(functools.partial(up_kernel, block_of(rows, 256)), out_sha...  18.4 us
  transfers between devices with their start and end apart: 11, of which 4 were waited for; matrix products, arithmetic and copies ran while one was open for 26% of the time, Pallas kernels for 37%

commit v1 on v0

--- a/solution.py
+++ b/solution.py
@@ -357,27 +357,49 @@
     return jnp.where(row < 4, left + right, jnp.maximum(left, right))
 
 
-def scatter_kernel(fsdp, tp, count, *refs):
-    parts = refs[:count]
-    small_ref = refs[count]
-    outs = refs[count + 1 : 2 * count + 1 - (tp - 1)]
-    small_out = refs[2 * count + 1 - (tp - 1)]
-    scratch = refs[2 * count + 2 - (tp - 1) :]
-    from_core, sum_core, from_side, sum_side, from_line, wide = (
-        scratch[n * count : (n + 1) * count] for n in range(6)
-    )
+def finish_kernel(fsdp, tp, *refs):
+    out_parts = refs[:tp]
+    normed = refs[tp : 2 * tp]
+    sent_rows = refs[2 * tp : 3 * tp - 1]
     (
+        grad_ref,
+        w_ref,
+        frames_ref,
+        hidden_ref,
+        gain_ref,
+        small_ref,
+        out_sum,
+        query_sum,
+        key_sum,
+        value_sum,
+        small_out,
+        rows_out,
+        turned,
+        made_q,
+        made_k,
+        made_v,
+        from_core,
+        from_side,
+        sum_side,
+        from_line,
         to_rank,
         from_rank,
+        got_rows,
         small_sum,
         small_got,
         core_sem,
         side_sem,
         line_sem,
         rank_sem,
+        rows_sem,
         small_sem,
-    ) = scratch[6 * count :]
+    ) = refs[3 * tp - 1 :]
     outer, middle, inner = split_place(fsdp)
+    own = frames_ref.shape[0]
+    width = made_q.shape[-1]
+    rows = made_q.shape[-2]
+    parts = [*out_parts, made_q, made_k, made_v]
+    count = len(parts)
     spot = lax.axis_index("fsdp")
     rank = lax.axis_index("tp")
     core = lax.rem(spot, inner)
@@ -404,6 +426,7 @@
             barrier, inc=1, device_id={"tp": peer}, device_id_type=pl.DeviceIdType.MESH
         )
     pl.semaphore_wait(barrier, len(lines) + len(sides) + len(cores) + len(ranks))
+    every = []
 
     def send(source, target, sems, axis, peer):
         copy = pltpu.make_async_remote_copy(
@@ -415,217 +438,298 @@
             device_id_type=pl.DeviceIdType.MESH,
         )
         copy.start()
+        every.append(copy)
         return copy
 
-    small_copies = []
-
-    def small_stage(first, axis, peers, source):
-        for index, peer in enumerate(peers):
-            number = first + index
-            small_copies.append(
-                send(source, small_got.at[number], small_sem.at[number], axis, peer)
-            )
-
-    def small_merge(first, peers, current, merge):
-        for index in range(len(peers)):
-            small_copies[first + index].wait_recv()
-            current = merge(current, small_got[first + index])
-        return current
-
-    small_stage(0, "fsdp", cores, small_ref)
-    core_copies = [
-        [
+    def send_core(index):
+        return [
             send(
-                part.at[:, core_steps[step]],
-                from_core[index].at[step],
+                parts[index].at[:, :, core_steps[step]],
+                from_core.at[index, step],
                 core_sem.at[index, step],
                 "fsdp",
                 cores[step],
             )
             for step in range(inner - 1)
         ]
-        for index, part in enumerate(parts)
+
+    def send_side(index, copies):
+        for copy in copies:
+            copy.wait_recv()
+
+        def add(n, carry):
+            new_line, new_side = lax.div(n, middle), lax.rem(n, middle)
+            value = parts[index][new_line, new_side, core].astype(WIDE)
+            for step in range(inner - 1):
+                value = value + from_core[index, step, new_line, new_side].astype(WIDE)
+            from_core[index, 0, new_line, new_side] = value.astype(LOW)
+            return carry
+
+        lax.fori_loop(0, outer * middle, add, 0)
+        return [
+            send(
+                from_core.at[index, 0, :, side_steps[step]],
+                from_side.at[index, step],
+                side_sem.at[index, step],
+                "fsdp",
+                sides[step],
+            )
+            for step in range(middle - 1)
+        ]
+
+    def send_line(index, copies):
+        for copy in copies:
+            copy.wait_recv()
+
+        def add(n, carry):
+            value = from_core[index, 0, n, side].astype(WIDE)
+            for step in range(middle - 1):
+                value = value + from_side[index, step, n].astype(WIDE)
+            sum_side[index, n] = value.astype(LOW)
+            return carry
+
+        lax.fori_loop(0, outer, add, 0)
+        return [
+            send(
+                sum_side.at[index, line_steps[step]],
+                from_line.at[index, step],
+                line_sem.at[index, step],
+                "fsdp",
+                lines[step],
+            )
+            for step in range(outer - 1)
+        ]
+
+    def finish(index, copies):
+        value = sum_side[index, line].astype(WIDE)
+        for step in range(outer - 1):
+            copies[step].wait_recv()
+            value = value + from_line[index, step].astype(WIDE)
+        return value
+
+    small_copies = []
+
+    def small_stage(axis, peers, source):
+        for peer in peers:
+            number = len(small_copies)
+            small_copies.append(
+                send(source, small_got.at[number], small_sem.at[number], axis, peer)
+            )
+
+    def small_merge(peers, current, merge):
+        first = len(small_copies) - len(peers)
+        for number in range(first, len(small_copies)):
+            small_copies[number].wait_recv()
+            current = merge(current, small_got[number])
+        return current
+
+    def make(target, number):
+        total = lax.dot_general(
+            turned[...],
+            grad_ref[number * width : (number + 1) * width, :],
+            (((1,), (1,)), ((), ())),
+            preferred_element_type=WIDE,
+        )
+        for block in range(outer * middle * inner):
+            spots = (block // (middle * inner), block // inner % middle, block % inner)
+            target[spots] = total[block * rows : (block + 1) * rows].astype(LOW)
+
+    def unit_of(chunk):
+        value = frames_ref[chunk, :].astype(WIDE)
+        centered = value - jnp.mean(value, axis=1, keepdims=True)
+        spread = jnp.mean(centered * centered, axis=1, keepdims=True)
+        inverse = lax.rsqrt(spread + NORM_EPSILON)
+        return centered * inverse, inverse
+
+    row_copies = [
+        send(
+            sent_rows[step - 1],
+            got_rows.at[step - 1],
+            rows_sem.at[step - 1],
+            "tp",
+            ranks[step - 1],
+        )
+        for step in range(1, tp)
     ]
-    total = small_merge(0, cores, small_ref[...], merge_rows)
+    core_copies = [send_core(index) for index in range(tp)]
+    for rows_value, place in row_chunks(normed, own):
+        turned[:, place] = rows_value.T
+    side_copies = [send_side(index, core_copies[index]) for index in range(tp)]
+    make(made_q, 0)
+    core_copies.append(send_core(tp))
+    make(made_k, 1)
+    core_copies.append(send_core(tp + 1))
+    side_copies.append(send_side(tp, core_copies[tp]))
+    make(made_v, 2)
+    core_copies.append(send_core(tp + 2))
+    side_copies.append(send_side(tp + 1, core_copies[tp + 1]))
+    line_copies = [send_line(index, side_copies[index]) for index in range(tp)]
+
+    step_rows = block_of(own, 256)
+    chunks = [slice(first, first + step_rows) for first in range(0, own, step_rows)]
+    gain_sum = small_ref[0:1, :]
+    bias_sum = small_ref[2:3, :]
+    for chunk in chunks:
+        grads = lax.dot_general(
+            grad_ref[:, chunk].T,
+            w_ref[...],
+            (((1,), (1,)), ((), ())),
+            preferred_element_type=WIDE,
+        )
+        rows_out[chunk, :] = grads
+        unit, _ = unit_of(chunk)
+        gain_sum = gain_sum + jnp.sum(grads * unit, axis=0, keepdims=True)
+        bias_sum = bias_sum + jnp.sum(grads, axis=0, keepdims=True)
+    side_copies.append(send_side(tp + 2, core_copies[tp + 2]))
+    line_copies.append(send_line(tp, side_copies[tp]))
+    row = lax.broadcasted_iota(jnp.int32, small_ref.shape, 0)
+    total = jnp.where(row == 0, gain_sum, jnp.where(row == 2, bias_sum, small_ref[...]))
     small_sum[0] = total
-    first_small = len(cores)
-    small_stage(first_small, "fsdp", sides, small_sum.at[0])
-
-    side_copies = []
-    for index, part in enumerate(parts):
-        for copy in core_copies[index]:
-            copy.wait_recv()
-
-        def add_core(n, carry, index=index, part=part):
-            value = part[n, core].astype(WIDE)
-            for step in range(inner - 1):
-                value = value + from_core[index][step, n].astype(WIDE)
-            sum_core[index][lax.div(n, middle), lax.rem(n, middle)] = value.astype(LOW)
-            return carry
-
-        lax.fori_loop(0, outer * middle, add_core, 0)
-        side_copies.append(
-            [
-                send(
-                    sum_core[index].at[:, side_steps[step]],
-                    from_side[index].at[step],
-                    side_sem.at[index, step],
-                    "fsdp",
-                    sides[step],
-                )
-                for step in range(middle - 1)
-            ]
-        )
-    total = small_merge(first_small, sides, total, merge_rows)
+    small_stage("fsdp", cores, small_sum.at[0])
+
+    total = small_merge(cores, total, merge_rows)
     small_sum[1] = total
-    first_small += len(sides)
-    small_stage(first_small, "fsdp", lines, small_sum.at[1])
-
-    line_copies = []
-    for index in range(count):
-        for copy in side_copies[index]:
-            copy.wait_recv()
-
-        def add_side(n, carry, index=index):
-            value = sum_core[index][n, side].astype(WIDE)
-            for step in range(middle - 1):
-                value = value + from_side[index][step, n].astype(WIDE)
-            sum_side[index][n] = value.astype(LOW)
-            return carry
-
-        lax.fori_loop(0, outer, add_side, 0)
-        line_copies.append(
-            [
-                send(
-                    sum_side[index].at[line_steps[step]],
-                    from_line[index].at[step],
-                    line_sem.at[index, step],
-                    "fsdp",
-                    lines[step],
-                )
-                for step in range(outer - 1)
-            ]
-        )
-    total = small_merge(first_small, lines, total, merge_rows)
+    small_stage("fsdp", sides, small_sum.at[1])
+    rank_copies = []
+    for index in range(1, tp):
+        to_rank[index - 1] = finish(index, line_copies[index]).astype(LOW)
+        rank_copies.append(
+            send(
+                to_rank.at[index - 1],
+                from_rank.at[index - 1],
+                rank_sem.at[index - 1],
+                "tp",
+                ranks[index - 1],
+            )
+        )
+    for index in range(tp + 1, count):
+        line_copies.append(send_line(index, side_copies[index]))
+    total = small_merge(sides, total, merge_rows)
     small_sum[2] = total
-    first_small += len(lines)
-    small_stage(first_small, "tp", ranks, small_sum.at[2])
-
-    rank_copies = []
-    for index in range(count):
-        value = sum_side[index][line].astype(WIDE)
-        for step in range(outer - 1):
-            line_copies[index][step].wait_recv()
-            value = value + from_line[index][step].astype(WIDE)
-        wide[index][...] = value
-        if 0 < index < tp:
-            to_rank[index - 1] = value.astype(LOW)
-            rank_copies.append(
-                send(
-                    to_rank.at[index - 1],
-                    from_rank.at[index - 1],
-                    rank_sem.at[index - 1],
-                    "tp",
-                    ranks[index - 1],
-                )
-            )
-    value = wide[0][...]
+    small_stage("fsdp", lines, small_sum.at[2])
+
+    for copy in row_copies:
+        copy.wait_recv()
+    for chunk in chunks:
+        grads = rows_out[chunk, :]
+        for step in range(tp - 1):
+            grads = grads + got_rows[step, chunk, :].astype(WIDE)
+        unit, inverse = unit_of(chunk)
+        scaled = grads * gain_ref[...]
+        mean = jnp.mean(scaled, axis=1, keepdims=True)
+        dot_unit = jnp.mean(scaled * unit, axis=1, keepdims=True)
+        rows_out[chunk, :] = hidden_ref[chunk, :] + inverse * (scaled - mean - unit * dot_unit)
+
+    total = small_merge(lines, total, merge_rows)
+    small_sum[3] = total
+    small_stage("tp", ranks, small_sum.at[3])
+    for index, target in zip(range(tp, count), (query_sum, key_sum, value_sum)):
+        target[...] = finish(index, line_copies[index])
+    value = finish(0, line_copies[0])
     for index, copy in enumerate(rank_copies):
         copy.wait_recv()
         value = value + from_rank[index].astype(WIDE)
-    outs[0][...] = value
-    for index in range(tp, count):
-        outs[index - tp + 1][...] = wide[index][...]
+    out_sum[...] = value
     small_out[...] = small_merge(
-        first_small,
         ranks,
         total,
-        lambda left, right: jnp.where(
-            lax.broadcasted_iota(jnp.int32, left.shape, 0) < 4, left + right, left
-        ),
+        lambda left, right: jnp.where(row < 4, left + right, left),
     )
-    for copies in (*core_copies, *side_copies, *line_copies, rank_copies, small_copies):
-        for copy in copies:
-            copy.wait_send()
-
-
-def scatter_end(parts, small, fsdp):
+    for copy in every:
+        copy.wait_send()
+
+
+def finish_step(out_parts, normed, sent_rows, grads, weights, frames, hidden, gain, small, fsdp):
     tp = lax.axis_size("tp")
     outer, middle, inner = split_place(fsdp)
-    count = len(parts)
-    rows = parts[0].shape[0] // fsdp
-    width = parts[0].shape[1]
-    shaped = [part.reshape(outer * middle, inner, rows, width) for part in parts]
+    rows = out_parts[0].shape[0] // fsdp
+    width = out_parts[0].shape[1]
+    padded = grads.shape[1]
+    depth = frames.shape[1]
+    out_parts = [part.reshape(outer, middle, inner, rows, width) for part in out_parts]
     in_vmem = pl.BlockSpec(memory_space=pltpu.VMEM)
+    count = tp + 3
     peers = (inner - 1) + (middle - 1) + (outer - 1) + (tp - 1)
 
-    def per_part(*shape, dtype=LOW):
-        return [pltpu.VMEM((*shape, rows, width), dtype)] * count
+    def low(*shape):
+        return pltpu.VMEM(shape, LOW)
 
     dma = pltpu.SemaphoreType.DMA
-    results = count - (tp - 1)
+    arguments = (*out_parts, *normed, *sent_rows, grads, weights, frames, hidden, gain[None], small)
     return pl.pallas_call(
-        functools.partial(scatter_kernel, fsdp, tp, count),
+        functools.partial(finish_kernel, fsdp, tp),
         out_shape=(
-            *[jax.ShapeDtypeStruct((rows, width), WIDE)] * results,
+            *[jax.ShapeDtypeStruct((rows, width), WIDE)] * 4,
             jax.ShapeDtypeStruct(small.shape, WIDE),
-        ),
-        in_specs=[in_vmem] * (count + 1),
-        out_specs=[in_vmem] * (results + 1),
+            jax.ShapeDtypeStruct(frames.shape, WIDE),
+        ),
+        in_specs=[in_vmem] * len(arguments),
+        out_specs=[in_vmem] * 6,
         scratch_shapes=[
-            *per_part(inner - 1, outer * middle),
-            *per_part(outer, middle),
-            *per_part(middle - 1, outer),
-            *per_part(outer),
-            *per_part(outer - 1),
-            *per_part(dtype=WIDE),
-            pltpu.VMEM((tp - 1, rows, width), LOW),
-            pltpu.VMEM((tp - 1, rows, width), LOW),
-            pltpu.VMEM((3, *small.shape), WIDE),
+            low(depth, padded),
+            *[low(outer, middle, inner, rows, width)] * 3,
+            low(count, inner - 1, outer, middle, rows, width),
+            low(count, middle - 1, outer, rows, width),
+            low(count, outer, rows, width),
+            low(count, outer - 1, rows, width),
+            low(tp - 1, rows, width),
+            low(tp - 1, rows, width),
+            low(tp - 1, *frames.shape),
+            pltpu.VMEM((4, *small.shape), WIDE),
             pltpu.VMEM((peers, *small.shape), WIDE),
             dma((count, inner - 1, 2)),
             dma((count, middle - 1, 2)),
             dma((count, outer - 1, 2)),
             dma((tp - 1, 2)),
+            dma((tp - 1, 2)),
             dma((peers, 2)),
         ],
         compiler_params=pltpu.CompilerParams(
-            collective_id=1, has_side_effects=True, vmem_limit_bytes=VMEM_BYTES
-        ),
-        name="scatter_end",
+            collective_id=1, has_side_effects=True, vmem_limit_bytes=63 * 2**20
+        ),
+        name="finish_step",
         cost_estimate=pl.CostEstimate(
-            flops=0, transcendentals=0, bytes_accessed=2 * count * fsdp * rows * width
-        ),
-    )(*shaped, small)
-
-
-def up_kernel(chunk, x_ref, w_ref, act_ref, slope_ref):
-    for first in range(0, x_ref.shape[0], chunk):
-        rows = slice(first, first + chunk)
-        pre = jnp.dot(x_ref[rows, :], w_ref[...], preferred_element_type=WIDE)
+            flops=8 * depth * width * padded, transcendentals=0, bytes_accessed=40 * 2**20
+        ),
+    )(*arguments)
+
+
+def block_of(size, wanted):
+    return wanted if size % wanted == 0 else size
+
+
+def row_chunks(pieces, wanted):
+    place = 0
+    for piece in pieces:
+        rows = piece.shape[0]
+        chunk = block_of(rows, wanted)
+        for first in range(0, rows, chunk):
+            yield piece[first : first + chunk, :], slice(place + first, place + first + chunk)
+        place += rows
+
+
+def up_kernel(parts, *refs):
+    w_ref, act_ref, slope_ref = refs[parts:]
+    for rows, place in row_chunks(refs[:parts], 256):
+        pre = jnp.dot(rows, w_ref[...], preferred_element_type=WIDE)
         scaled = pre * (2**-0.5)
         share = 0.5 + 0.5 * lax.erf(scaled)
         bell = jnp.exp2(scaled * scaled * -math.log2(math.e) - 0.5 * math.log2(2 * math.pi))
-        act_ref[rows, :] = (pre * share).astype(LOW)
-        slope_ref[rows, :] = (share + pre * bell).astype(LOW)
-
-
-def block_of(size, wanted):
-    return wanted if size % wanted == 0 else size
-
-
-def up_and_gelu(x, weights, units):
-    rows, depth = x.shape
+        act_ref[place, :] = (pre * share).astype(LOW)
+        slope_ref[place, :] = (share + pre * bell).astype(LOW)
+
+
+def up_and_gelu(pieces, weight):
+    rows = sum(piece.shape[0] for piece in pieces)
+    depth, units = weight.shape
     block = block_of(units, 512)
     shape = jax.ShapeDtypeStruct((rows, units), LOW)
     return pl.pallas_call(
-        functools.partial(up_kernel, block_of(rows, 256)),
+        functools.partial(up_kernel, len(pieces)),
         out_shape=(shape, shape),
         grid=(units // block,),
-        in_specs=[
-            whole_block((rows, depth)),
-            pl.BlockSpec((depth, block), lambda j: (0, j)),
-        ],
+        in_specs=[whole_block(piece.shape) for piece in pieces]
+        + [pl.BlockSpec((depth, block), lambda j: (0, j))],
         out_specs=[pl.BlockSpec((rows, block), lambda j: (0, j))] * 2,
         compiler_params=pltpu.CompilerParams(vmem_limit_bytes=VMEM_BYTES),
         name="up_and_gelu",
@@ -634,19 +738,57 @@
             transcendentals=2 * rows * units,
             bytes_accessed=2 * (rows * depth + depth * units + 2 * rows * units),
         ),
-    )(x, weights)
-
-
-def weight_kernel(steps, left_a, right_a, left_b, right_b, out_ref, turned):
+    )(*pieces, weight)
+
+
+def slope_kernel(parts, *refs):
+    w_ref, slope_ref, out_ref = refs[parts:]
+    for rows, place in row_chunks(refs[:parts], 512):
+        grad = jnp.dot(rows, w_ref[...], preferred_element_type=WIDE)
+        out_ref[place, :] = (grad * slope_ref[place, :].astype(WIDE)).astype(LOW)
+
+
+def times_slope(pieces, weight, slope):
+    rows, units = slope.shape
+    depth = weight.shape[0]
+    block = block_of(units, 512)
+    return pl.pallas_call(
+        functools.partial(slope_kernel, len(pieces)),
+        out_shape=jax.ShapeDtypeStruct((rows, units), LOW),
+        grid=(units // block,),
+        in_specs=[whole_block(piece.shape) for piece in pieces]
+        + [
+            pl.BlockSpec((depth, block), lambda j: (0, j)),
+            pl.BlockSpec((rows, block), lambda j: (0, j)),
+        ],
+        out_specs=pl.BlockSpec((rows, block), lambda j: (0, j)),
+        compiler_params=pltpu.CompilerParams(vmem_limit_bytes=VMEM_BYTES),
+        name="times_slope",
+        cost_estimate=pl.CostEstimate(
+            flops=2 * rows * depth * units,
+            transcendentals=0,
+            bytes_accessed=2 * (rows * depth + depth * units + 2 * rows * units),
+        ),
+    )(*pieces, weight, slope)
+
+
+def weight_kernel(steps, parts_a, parts_b, *refs):
+    left_a = refs[:parts_a]
+    left_b = refs[parts_a : parts_a + parts_b]
+    right_a, right_b, out_ref, turned = refs[parts_a + parts_b :]
     step = pl.program_id(0)
+
+    def turn(pieces):
+        for rows, place in row_chunks(pieces, pieces[0].shape[0]):
+            turned[:, place] = rows.T
 
     @pl.when(step == 0)
     def _():
-        turned[...] = left_a[...].T
+        turn(left_a)
 
     @pl.when(step == steps)
     def _():
-        turned[...] = left_b[...].T
+        turn(left_b)
 
     @pl.when(step < steps)
     def _():
@@ -662,18 +804,17 @@
 
 
 def two_weight_grads(left_a, right_a, left_b, right_b):
-    rows, depth = left_a.shape
-    units = right_a.shape[1]
+    rows, units = right_a.shape
+    depth = left_a[0].shape[1]
     block = block_of(units, 512)
     steps = units // block
     return pl.pallas_call(
-        functools.partial(weight_kernel, steps),
+        functools.partial(weight_kernel, steps, len(left_a), len(left_b)),
         out_shape=jax.ShapeDtypeStruct((depth, 2 * units), LOW),
         grid=(2 * steps,),
-        in_specs=[
-            whole_block((rows, depth)),
+        in_specs=[whole_block(piece.shape) for piece in (*left_a, *left_b)]
+        + [
             pl.BlockSpec((rows, block), lambda j: (0, jnp.minimum(j, steps - 1))),
-            whole_block((rows, depth)),
             pl.BlockSpec((rows, block), lambda j: (0, jnp.maximum(j - steps, 0))),
         ],
         out_specs=pl.BlockSpec((depth, block), lambda j: (0, j)),
@@ -681,11 +822,11 @@
         compiler_params=pltpu.CompilerParams(vmem_limit_bytes=VMEM_BYTES),
         name="two_weight_grads",
         cost_estimate=pl.CostEstimate(
-            flops=6 * rows * depth * units,
+            flops=4 * rows * depth * units,
             transcendentals=0,
             bytes_accessed=4 * (rows * depth + depth * units + rows * units),
         ),
-    )(left_a, right_a, left_b, right_b)
+    )(*left_a, *left_b, right_a, right_b)
 
 
 def norm_parts(rows):
@@ -768,11 +909,9 @@
     info = jnp.stack([length, me * own, jnp.int32(padded)]).astype(jnp.int32)
 
     shard_qkv = jnp.concatenate([w_query, w_key, w_value], axis=1)
-    shard_rest = jnp.concatenate([w_up, w_down.T], axis=1)
     qkv_blocks, out_blocks, other_frames = gather_start(shard_qkv, w_output.T, own_frames, fsdp)
-    w_rest = gather(after(shard_rest, other_frames))
-    full_up = w_rest[:, :units]
-    down_t = w_rest[:, units:]
+    full_up = gather(w_up)
+    down_t = gather(after(w_down.T, other_frames))
     w_qkv = qkv_blocks.reshape(-1, 3 * cols)
     out_pieces = [out_blocks[j].reshape(-1, cols) for j in range(tp)]
     other_frames = [other_frames[s] for s in range(tp - 1)]
@@ -825,13 +964,12 @@
     for piece in hidden_pieces:
         unit, _ = norm_parts(piece)
         normed_two_pieces.append((unit * norm_gains[1] + norm_biases[1]).astype(LOW))
-    normed_two = jnp.concatenate(normed_two_pieces, axis=0)
     hidden_own = hidden_pieces[0]
-    activated, slope = up_and_gelu(normed_two, w_rest, units)
+    activated, slope = up_and_gelu(normed_two_pieces, full_up)
 
     other_cotans = [piece for pair in zip(early_cotans, late_cotans) for piece in pair]
-    cotan_all = jnp.concatenate([cotan, *other_cotans], axis=0)
-    grad_pre = (dot(cotan_all, down_t) * slope.astype(WIDE)).astype(LOW)
+    cotan_pieces = [cotan, *other_cotans]
+    grad_pre = times_slope(cotan_pieces, down_t, slope)
 
     def rows_of(value, j):
         return value[j * own : (j + 1) * own]
@@ -841,7 +979,7 @@
     ]
     received_two = exchange(sent_two)
     gate = after(grad_pre, sent_two[1:])
-    total_rest = two_weight_grads(normed_two, gate, cotan_all, activated)
+    total_rest = two_weight_grads(normed_two_pieces, gate, cotan_pieces, activated)
     rest_sum = scatter(total_rest)
     own_two = dot(rows_of(after(gate, total_rest), 0), full_up, 1, 1)
     received_two = [after(item, own_two) for item in received_two]
@@ -874,35 +1012,30 @@
     sent_one = [None] + [
         dot(columns_of(grad_qkv, j), w_qkv, 0, 1).astype(LOW) for j in range(1, tp)
     ]
-    received_one = exchange(sent_one)
-    gate = after(grad_qkv, sent_one[1:])
-    total_qkv = [
-        dot(normed_all, gate[n * cols : (n + 1) * cols], 0, 1).astype(LOW) for n in range(3)
-    ]
-    own_one = dot(columns_of(gate, 0), w_qkv, 0, 1)
-    frames_late = [after(piece, grad_qkv) for piece in frame_pieces]
-    units_one = [norm_parts(piece.astype(WIDE)) for piece in frames_late]
-    gain_one = jnp.sum(own_one * units_one[0][0], axis=0)
-    bias_one = jnp.sum(own_one, axis=0)
+    gain_one = jnp.zeros_like(gain_two)
+    bias_one = gain_one
     for j in range(1, tp):
+        unit, _ = norm_parts(after(frame_pieces[j], grad_qkv).astype(WIDE))
         part = sent_one[j].astype(WIDE)
-        gain_one = gain_one + jnp.sum(part * units_one[j][0], axis=0)
+        gain_one = gain_one + jnp.sum(part * unit, axis=0)
         bias_one = bias_one + jnp.sum(part, axis=0)
-
     head_top = jnp.concatenate(tops, axis=0)[:, 0] * SCORE_SCALE
     head_row = jnp.pad(head_top, (0, gain_one.shape[0] - heads))
     blank = jnp.zeros_like(head_row)
     small = jnp.stack([gain_one, gain_two, bias_one, bias_two, head_row, blank, blank, blank])
-    out_sum, query_sum, key_sum, value_sum, small = scatter_end(
-        [*total_out, *total_qkv], small, fsdp
+    out_sum, query_sum, key_sum, value_sum, small, grad_frames = finish_step(
+        total_out,
+        normed_pieces,
+        sent_one[1:],
+        grad_qkv,
+        w_qkv,
+        own_frames,
+        grad_hidden,
+        norm_gains[0],
+        small,
+        fsdp,
     )
     head_top = small[4, :heads]
-    received_one = [after(item, small) for item in received_one]
-    grad_normed_one = own_one
-    for item in received_one:
-        grad_normed_one = grad_normed_one + item.astype(WIDE)
-    grad_from_one, _, _ = norm_backward(grad_normed_one, *units_one[0], norm_gains[0])
-    grad_frames = grad_hidden + grad_from_one
     output = hidden_own + sent_mlp[0]
     for item in received_mlp:
         output = output + item.astype(WIDE)

time: 511 us -> 535 us (1.047)
  Pallas kernels: 264 us -> 322 us
  matrix products: 113 us -> 75.6 us
  waiting for transfers between devices: 42.2 us -> 56.9 us
  other arithmetic: 45.5 us -> 34.4 us
    pallas_call x3 -> x4, Pallas kernels: 119 us -> 157 us  [the longest x1 92.6 us: finish_step(): pl.pallas_call(functools.partial(finish_kernel, fsdp, tp), out_shape=(*[j...]
    dot_general x20 -> x15, matrix products: 113 us -> 75.6 us  [dot(): lax.dot_general(left, right, (((left_dim,), (right_dim,)), ((), ())), pre...]
    pallas_call x1, Pallas kernels: 60.2 us -> 80.7 us  [gather_start(): pl.pallas_call(functools.partial(gather_kernel, fsdp, tp), out_shape=(jax...]
    ppermute x9 -> x8, waiting for transfers between devices: 42.2 us -> 56.1 us  [shift(): return lax.ppermute(value, 'tp', pairs)]
    concatenate x3 -> x0, other arithmetic: 6.53 us -> none  [the longest x1 2.2 us: on_device(): shard_rest = jnp.concatenate([w_up, w_down.T], axis=1)]
    unnamed x118 -> x83, local copies, waits for them, and re-layouts: 10.7 us -> 7.97 us
  transfers between devices with their start and end apart: 11 -> 11, of which waited for: 4 -> 3; matrix products, arithmetic and copies ran while one was open for 26% -> 20% of each run, Pallas kernels for 37% -> 52%
where the time goes in v1:
time: 535 us; the launch traced here: 529 us
  Pallas kernels  322 us (60%)
  matrix products  75.6 us (14%)
  waiting for transfers between devices  56.9 us (11%)
  other arithmetic  34.4 us (6%)
  local copies, waits for them, and re-layouts  18.3 us (3%)
  between operations  14.7 us (3%)
  starting transfers between devices  7.49 us (1%)
    pallas_call x1, Pallas kernels, finish_step(): pl.pallas_call(functools.partial(finish_kernel, fsdp, tp), out_shape=(*[j...  92.6 us
    pallas_call x1, Pallas kernels, gather_start(): pl.pallas_call(functools.partial(gather_kernel, fsdp, tp), out_shape=(jax...  80.7 us
    dot_general x15, matrix products, dot(): lax.dot_general(left, right, (((left_dim,), (right_dim,)), ((), ())), pre...  75.6 us
    ppermute x8, waiting for transfers between devices, shift(): return lax.ppermute(value, 'tp', pairs)  56.1 us
    pallas_call x1, Pallas kernels, attention_backward(): pl.pallas_call(functools.partial(backward_kernel, len(pieces)), out_shape...  51 us
    pallas_call x3, Pallas kernels, attention_forward(): pl.pallas_call(functools.partial(forward_kernel, len(pieces)), out_shape=...  33.5 us
    pallas_call x1, Pallas kernels, two_weight_grads(): pl.pallas_call(functools.partial(weight_kernel, steps, len(left_a), len(l...  30 us
    pallas_call x1, Pallas kernels, up_and_gelu(): pl.pallas_call(functools.partial(up_kernel, len(pieces)), out_shape=(shap...  18.4 us
  transfers between devices with their start and end apart: 11, of which 3 were waited for; matrix products, arithmetic and copies ran while one was open for 20% of the time, Pallas kernels for 52%

profile of v1, /device:TPU:0, one launch (start us, length us, event | category | flops | bytes accessed | tf_op | source)
XLA Modules:
  0.0 529.4 jit_solution(566067327482314191)
XLA Ops:
  7.2 0.7 all-gather.3.cloned.1.call-update
  8.0 1.7 pad_maximum_fusion.3.shard_qkv
  9.7 80.7 %gather_start.1 = (bf16[16,80,1920]{2,1,0:T(8,128)(2,1)}, bf16[2,16,80,640]{3,2,1,0:T(8,128)(2,1)}, bf16[1,768,1280]{2,1,0:T(8,128)(2,1)}) custom-call(bf16[80,1920]{1,0:T(8,128)(2,1)} %pad_maximum_fusion.3.shard_qkv, bf16[80,640]{1,0:T(8,128)(2,1)} %bitcast.74, bf16[768,1280]{1,0:T(8,128)(2,1)} %bitcast.61), custom_call_target="tpu_custom_call" | custom-call | bytes 6553600 | tf_op jit(solution)/shard_map/gather_start/pallas_call | solution.py:331
  90.5 2.0 convert_reduce_fusion
  92.5 1.9 convert_reduce_fusion.1
  94.5 0.6 fusion.6
  95.1 0.6 slice_reduce_fusion.1
  95.8 2.2 fusion.10
  98.0 0.6 fusion.49
  98.6 1.2 pad_add_fusion.info_ref
  99.9 9.0 %convolution_convert_fusion.1.refs_1_.refs_3_.refs_5_ = bf16[1920,768]{1,0:T(8,128)(2,1)} fusion(bf16[1280,1920]{1,0:T(8,128)(2,1)} %bitcast.77, bf16[1,768,1280]{2,1,0:T(8,128)(2,1)S(1)} %copy-done.2, f32[768]{0:T(1024)S(1)} %add_rsqrt_fusion.3, f32[768]{0:T(1024)S(1)} %broadcast_multiply_fusion.5, f32[1280]{0:T(1024)S(1)} %get-tuple-element.87, ...), kind=kOutput, calls=%fused_computation.51 | convolution fusion | flops 3782246400 | bytes 9846784 | tf_op jit(solution)/shard_map/dot_general | solution.py:851
  108.8 8.5 %convolution_convert_fusion.2.refs_0_.refs_2_.refs_4_ = bf16[1920,768]{1,0:T(8,128)(2,1)} fusion(bf16[1280,1920]{1,0:T(8,128)(2,1)} %bitcast.78, bf16[1,768,1280]{2,1,0:T(8,128)(2,1)S(1)} %copy-done.3, f32[1280]{0:T(1024)S(1)} %get-tuple-element.87, f32[1280]{0:T(1024)S(1)} %get-tuple-element.85, f32[768]{0:T(1024)S(1)} %add_rsqrt_fusion.4, ...), kind=kOutput, calls=%fused_computation.52 | convolution fusion | flops 3782246400 | bytes 9846784 | tf_op jit(solution)/shard_map/dot_general | solution.py:851
  117.4 9.0 %attention_forward.3 = (bf16[160,1536]{1,0:T(8,128)(2,1)}, f32[2,1536]{1,0:T(2,128)}, f32[2,128]{1,0:T(2,128)}) custom-call(s32[3]{0:T(128)} %pad_add_fusion.info_ref, bf16[1920,768]{1,0:T(8,128)(2,1)} %convolution_convert_fusion.2.refs_0_.refs_2_.refs_4_, bf16[1920,768]{1,0:T(8,128)(2,1)} %convolution_convert_fusion.1.refs_1_.refs_3_.refs_5_, ...), custom_call_target="tpu_custom_call" | custom-call | flops 8455716864 | bytes 1966080 | tf_op jit(solution)/shard_map/attention_forward/pallas_call | solution.py:87
  126.4 1.6 collective-permute-start
  128.0 12.2 %attention_forward.4 = (bf16[240,1536]{1,0:T(8,128)(2,1)}, f32[3,1536]{1,0:T(4,128)}, f32[3,128]{1,0:T(4,128)}) custom-call(s32[3]{0:T(128)} %pad_add_fusion.info_ref, bf16[1920,768]{1,0:T(8,128)(2,1)} %convolution_convert_fusion.2.refs_0_.refs_2_.refs_4_, bf16[1920,768]{1,0:T(8,128)(2,1)} %convolution_convert_fusion.1.refs_1_.refs_3_.refs_5_, ...), custom_call_target="tpu_custom_call" | custom-call | flops 12683575296 | bytes 2949120 | tf_op jit(solution)/shard_map/attention_forward/pallas_call | solution.py:87
  140.6 12.3 %attention_forward.5 = (bf16[240,1536]{1,0:T(8,128)(2,1)}, f32[3,1536]{1,0:T(4,128)}, f32[3,128]{1,0:T(4,128)}) custom-call(s32[3]{0:T(128)} %pad_add_fusion.info_ref, bf16[1920,768]{1,0:T(8,128)(2,1)} %convolution_convert_fusion.2.refs_0_.refs_2_.refs_4_, bf16[1920,768]{1,0:T(8,128)(2,1)} %convolution_convert_fusion.1.refs_1_.refs_3_.refs_5_, ...), custom_call_target="tpu_custom_call" | custom-call | flops 12683575296 | bytes 2949120 | tf_op jit(solution)/shard_map/attention_forward/pallas_call | solution.py:87
  153.0 1.7 collective-permute-start.2
  154.7 2.9 slice_bitcast_fusion
  157.6 0.7 collective-permute-start.3
  158.8 2.4 copy-done.4
  161.2 1.7 convert_add_fusion.1
  163.0 1.7 convert_add_fusion
  164.8 10.8 %collective-permute-done.2 = bf16[240,1536]{1,0:T(8,128)(2,1)S(1)} collective-permute-done((bf16[240,1536]{1,0:T(8,128)(2,1)}, bf16[240,1536]{1,0:T(8,128)(2,1)S(1)}, u32[]{:S(2)}, u32[]{:S(2)}) %collective-permute-start.2) | collective-permute-done | bytes 737312 | tf_op jit(solution)/shard_map/ppermute | solution.py:891
  175.6 1.1 fusion.56
  177.3 1.9 fusion.61
  179.7 1.9 fusion.60
  181.6 0.5 multiply_reduce_fusion.2
  182.2 2.7 add_convert_fusion.1
  184.9 18.4 %up_and_gelu.1 = (bf16[1536,2560]{1,0:T(8,128)(2,1)}, bf16[1536,2560]{1,0:T(8,128)(2,1)}) custom-call(bf16[768,1280]{1,0:T(8,128)(2,1)} %get-tuple-element.105.refs_0_, bf16[768,1280]{1,0:T(8,128)(2,1)} %get-tuple-element.104.refs_1_, bf16[1280,2560]{1,0:T(8,128)(2,1)} %all-gather.3.cloned.1.call-done.refs_2_), custom_call_target="tpu_custom_call" | custom-call | flops 15099494400 | bytes 26214400 | tf_op jit(solution)/shard_map/up_and_gelu/pallas_call | solution.py:727
  203.3 13.9 %collective-permute-done.4.refs_2_.refs_4_ = bf16[384,1280]{1,0:T(8,128)(2,1)} collective-permute-done((bf16[384,1280]{1,0:T(8,128)(2,1)}, bf16[384,1280]{1,0:T(8,128)(2,1)}, u32[]{:S(2)}, u32[]{:S(2)}) %collective-permute-start.4) | collective-permute-done | bytes 983072 | tf_op jit(solution)/shard_map/ppermute | solution.py:891
  217.1 15.9 %times_slope.1.refs_5_ = bf16[1536,2560]{1,0:T(8,128)(2,1)} custom-call(bf16[768,1280]{1,0:T(8,128)(2,1)} %bitcast.66, bf16[384,1280]{1,0:T(8,128)(2,1)} %collective-permute-done.3.refs_1_.refs_3_, bf16[384,1280]{1,0:T(8,128)(2,1)} %collective-permute-done.4.refs_2_.refs_4_, bf16[1280,2560]{1,0:T(8,128)(2,1)} %all-gather.5.cloned.1.call-done.refs_3_, ...), custom_call_target="tpu_custom_call" | custom-call | flops 10066329600 | bytes 26214400 | tf_op jit(solution)/shard_map/times_slope/pallas_call | solution.py:755
  233.0 9.9 %fusion.24 = bf16[768,1280]{1,0:T(8,128)(2,1)} fusion(bf16[1280,2560]{1,0:T(8,128)(2,1)} %all-gather.3.cloned.1.call-done.refs_2_, bf16[1536,2560]{1,0:T(8,128)(2,1)} %times_slope.1.refs_5_), kind=kOutput, calls=%fused_computation.49 | convolution fusion | flops 5034147840 | bytes 12451840 | tf_op jit(solution)/shard_map/dot_general | solution.py:851
  243.0 30.0 %two_weight_grads.1 = bf16[1280,5120]{1,0:T(8,128)(2,1)} custom-call(bf16[768,1280]{1,0:T(8,128)(2,1)} %get-tuple-element.105.refs_0_, bf16[768,1280]{1,0:T(8,128)(2,1)} %get-tuple-element.104.refs_1_, bf16[768,1280]{1,0:T(8,128)(2,1)} %bitcast.67, bf16[384,1280]{1,0:T(8,128)(2,1)} %collective-permute-done.3.refs_1_.refs_3_, ...), custom_call_target="tpu_custom_call" | custom-call | flops 20132659200 | bytes 36700160 | tf_op jit(solution)/shard_map/two_weight_grads/pallas_call | solution.py:811
  273.0 0.6 copy-done.28
  273.9 0.6 pad_maximum_fusion.4.refs_9_
  274.9 4.2 fusion.9
  279.1 8.3 %fusion.22 = f32[768,1280]{1,0:T(8,128)S(1)} fusion(bf16[1280,2560]{1,0:T(8,128)(2,1)} %all-gather.3.cloned.1.call-done.refs_2_, bf16[1536,2560]{1,0:T(8,128)(2,1)S(1)} %copy-done.33), kind=kOutput, calls=%fused_computation.39 | convolution fusion | flops 5033164800 | bytes 14417920 | tf_op jit(solution)/shard_map/dot_general | solution.py:851
  287.4 31.5 %collective-permute-done.5 = bf16[768,1280]{1,0:T(8,128)(2,1)S(1)} collective-permute-done((bf16[768,1280]{1,0:T(8,128)(2,1)}, bf16[768,1280]{1,0:T(8,128)(2,1)S(1)}, u32[]{:S(2)}, u32[]{:S(2)}) %collective-permute-start.5) | collective-permute-done | bytes 1966112 | tf_op jit(solution)/shard_map/ppermute | solution.py:891
  318.9 2.1 multiply_reduce_fusion
  321.0 3.5 fusion.54
  324.5 1.5 convolution_convert_fusion.6
  326.5 2.9 convolution_convert_fusion.3
  329.4 2.9 convolution_convert_fusion.4
  332.3 2.5 convolution_convert_fusion.5.refs_6_
  334.8 7.2 %fusion.20 = f32[768,1280]{1,0:T(8,128)} fusion(bf16[1280,2560]{1,0:T(8,128)(2,1)S(1)} %bitcast.76, bf16[1536,2560]{1,0:T(8,128)(2,1)S(1)} %bitcast.86), kind=kOutput, calls=%fused_computation.34 | convolution fusion | flops 5033164800 | bytes 14417920 | tf_op jit(solution)/shard_map/dot_general | solution.py:851
  342.0 6.4 %fusion.18 = bf16[768,1280]{1,0:T(8,128)(2,1)} fusion(bf16[1280,2560]{1,0:T(8,128)(2,1)S(1)} %bitcast.76, bf16[1536,2560]{1,0:T(8,128)(2,1)S(1)} %bitcast.86), kind=kOutput, calls=%fused_computation.32 | convolution fusion | flops 5033164800 | bytes 12451840 | tf_op jit(solution)/shard_map/dot_general | solution.py:851
  348.5 51.0 %attention_backward.1 = bf16[3,640,1536]{2,1,0:T(8,128)(2,1)} custom-call(s32[3]{0:T(128)} %pad_add_fusion.info_ref, bf16[1920,768]{1,0:T(8,128)(2,1)} %convolution_convert_fusion.2.refs_0_.refs_2_.refs_4_, bf16[1920,768]{1,0:T(8,128)(2,1)} %convolution_convert_fusion.1.refs_1_.refs_3_.refs_5_, ...), custom_call_target="tpu_custom_call" | custom-call | flops 62813896704 | bytes 15728640 | tf_op jit(solution)/shard_map/attention_backward/pallas_call | solution.py:168
  399.5 1.7 collective-permute-start.7
  401.5 0.6 fusion.14
  402.1 9.3 %convert_reduce_fusion.3 = (f32[1280]{0:T(1024)S(1)}, f32[1280]{0:T(1024)S(1)}, bf16[768,1280]{1,0:T(8,128)(2,1)}) fusion(f32[768]{0:T(1024)S(1)} %add_rsqrt_fusion, f32[768]{0:T(1024)S(1)} %broadcast_multiply_fusion, bf16[768,1280]{1,0:T(8,128)(2,1)S(1)} %bitcast.60, bf16[1280,1920]{1,0:T(8,128)(2,1)} %bitcast.79, bf16[1920,1536]{1,0:T(8,128)(2,1)} %bitcast.81), kind=kOutput, calls=%fused_computation.8 | convolution fusion | flops 3782735360 | bytes 11812864 | tf_op jit(solution)/shard_map/dot_general | solution.py:851
  411.4 0.7 stack.39.refs_10_
  412.1 92.6 %finish_step.1 = (f32[80,640]{1,0:T(8,128)}, f32[80,640]{1,0:T(8,128)}, f32[80,640]{1,0:T(8,128)}, f32[80,640]{1,0:T(8,128)}, f32[8,1280]{1,0:T(8,128)}, /*index=5*/f32[768,1280]{1,0:T(8,128)}) custom-call(bf16[4,2,2,80,640]{4,3,2,1,0:T(8,128)(2,1)} %bitcast.84, bf16[4,2,2,80,640]{4,3,2,1,0:T(8,128)(2,1)} %bitcast.83, ...), custom_call_target="tpu_custom_call" | custom-call | flops 10066329600 | bytes 41943040 | tf_op jit(solution)/shard_map/finish_step/pallas_call | solution.py:659
  504.7 0.7 sqrt_bitcast_fusion
  505.6 0.8 convert_multiply_fusion.1
  506.4 1.5 fusion.59
  507.8 5.8 %fusion.32 = bf16[1,768,1280]{2,1,0:T(8,128)(2,1)} fusion(bf16[768,1280]{1,0:T(8,128)(2,1)} %collective-permute-done.7, f32[768,1280]{1,0:T(8,128)} %copy-done, f32[768,1280]{1,0:T(8,128)} %fusion.20), kind=kLoop, calls=%fused_computation.58 | loop fusion | flops 3932160 | bytes 11796480 | tf_op jit(solution)/shard_map/broadcast_in_dim | solution.py:1046
  513.6 1.4 convert_element_type.121
  515.1 0.9 slice_bitcast_fusion.2
  516.0 2.0 slice.132
  518.0 1.9 copy.31
  519.9 0.7 copy.32
  520.6 0.7 copy.33
  521.3 0.7 copy.34
  522.0 0.7 copy.35
  (125 shorter events, 3.8 us)
Async XLA Ops:
  7.2 177.7 %all-gather.3.cloned.1.call-start = ((), (), s32[]{:S(2)}) async-start(), calls=%async_computation.1 | async-start | bytes 6963200 | tf_op jit(solution)/shard_map/all_gather | solution.py:900
  7.9 209.2 %all-gather.5.cloned.1.call-start = ((), (), s32[]{:S(2)}) async-start(), calls=%async_computation.2 | async-start | bytes 6963200 | tf_op jit(solution)/shard_map/all_gather | solution.py:900
  9.7 85.4 %copy-start.26 = (f32[2,1280]{1,0:T(2,128)S(1)}, f32[2,1280]{1,0:T(2,128)}, u32[]{:S(2)}) copy-start(f32[2,1280]{1,0:T(2,128)} %param.20) | copy-start | bytes 30724
  9.7 86.0 %copy-start.27 = (f32[2,1280]{1,0:T(2,128)S(1)}, f32[2,1280]{1,0:T(2,128)}, u32[]{:S(2)}) copy-start(f32[2,1280]{1,0:T(2,128)} %param.21) | copy-start | bytes 30724
  90.4 4.0 copy-start.2
  90.4 7.6 %copy-start.31 = (s32[16]{0:T(128)S(1)}, s32[16]{0:T(128)}, u32[]{:S(2)}) copy-start(s32[16]{0:T(128)} %param.22) | copy-start | bytes 196
  90.4 7.6 %copy-start.32 = (s32[16]{0:T(128)S(1)}, s32[16]{0:T(128)}, u32[]{:S(2)}) copy-start(s32[16]{0:T(128)} %param.23) | copy-start | bytes 196
  90.5 423.2 %reduce-scatter.2.cloned.1.call-start = ((), (), s32[]{:S(2)}) async-start(), calls=%async_computation.3 | async-start | bytes 13926400 | tf_op jit(solution)/shard_map/reduce_scatter | solution.py:903
  99.9 9.0 %copy-start.3 = (bf16[1,768,1280]{2,1,0:T(8,128)(2,1)S(1)}, bf16[1,768,1280]{2,1,0:T(8,128)(2,1)}, u32[]{:S(2)}) copy-start(bf16[1,768,1280]{2,1,0:T(8,128)(2,1)} %param.12) | copy-start | bytes 5898244
  126.4 38.4 %collective-permute-start = (bf16[160,1536]{1,0:T(8,128)(2,1)}, bf16[160,1536]{1,0:T(8,128)(2,1)S(1)}, u32[]{:S(2)}, u32[]{:S(2)}) collective-permute-start(bf16[160,1536]{1,0:T(8,128)(2,1)} %get-tuple-element.47), channel_id=1, source_target_pairs={{1,0},{0,1},{3,2},{2,3},{5,4},{4,5},{7,6},{6,7},{9,8},{8,9},{11,10... | collective-permute-start | bytes 1474568 | tf_op jit(solution)/shard_map/ppermute | solution.py:891
  140.2 35.4 %collective-permute-start.1 = (bf16[240,1536]{1,0:T(8,128)(2,1)}, bf16[240,1536]{1,0:T(8,128)(2,1)}, u32[]{:S(2)}, u32[]{:S(2)}) collective-permute-start(bf16[240,1536]{1,0:T(8,128)(2,1)} %get-tuple-element.49), channel_id=1, source_target_pairs={{1,0},{0,1},{3,2},{2,3},{5,4},{4,5},{7,6},{6,7},{9,8},{8,9},{11,10... | collective-permute-start | bytes 2211848 | tf_op jit(solution)/shard_map/ppermute | solution.py:891
  152.9 5.4 %copy-start.14 = (bf16[160,1536]{1,0:T(8,128)(2,1)S(1)}, bf16[160,1536]{1,0:T(8,128)(2,1)}, u32[]{:S(2)}) copy-start(bf16[160,1536]{1,0:T(8,128)(2,1)} %get-tuple-element.47) | copy-start | bytes 1474564
  152.9 5.4 %copy-start.12 = (bf16[240,1536]{1,0:T(8,128)(2,1)S(1)}, bf16[240,1536]{1,0:T(8,128)(2,1)}, u32[]{:S(2)}) copy-start(bf16[240,1536]{1,0:T(8,128)(2,1)} %get-tuple-element.49) | copy-start | bytes 2211844
  153.0 5.4 %copy-start.13 = (bf16[240,1536]{1,0:T(8,128)(2,1)S(1)}, bf16[240,1536]{1,0:T(8,128)(2,1)}, u32[]{:S(2)}) copy-start(bf16[240,1536]{1,0:T(8,128)(2,1)} %get-tuple-element.51) | copy-start | bytes 2211844
  153.0 5.5 %copy-start.9 = (bf16[2,16,80,640]{3,2,1,0:T(8,128)(2,1)S(1)}, bf16[2,16,80,640]{3,2,1,0:T(8,128)(2,1)}, u32[]{:S(2)}) copy-start(bf16[2,16,80,640]{3,2,1,0:T(8,128)(2,1)} %get-tuple-element.52) | copy-start | bytes 9830404
  153.0 22.6 %collective-permute-start.2 = (bf16[240,1536]{1,0:T(8,128)(2,1)}, bf16[240,1536]{1,0:T(8,128)(2,1)S(1)}, u32[]{:S(2)}, u32[]{:S(2)}) collective-permute-start(bf16[240,1536]{1,0:T(8,128)(2,1)} %get-tuple-element.51), channel_id=1, source_target_pairs={{1,0},{0,1},{3,2},{2,3},{5,4},{4,5},{7,6},{6,7},{9,8},{8,9},{11,10... | collective-permute-start | bytes 2211848 | tf_op jit(solution)/shard_map/ppermute | solution.py:891
  157.6 45.7 %collective-permute-start.3 = (bf16[384,1280]{1,0:T(8,128)(2,1)}, bf16[384,1280]{1,0:T(8,128)(2,1)}, u32[]{:S(2)}, u32[]{:S(2)}) collective-permute-start(bf16[384,1280]{1,0:T(8,128)(2,1)} %get-tuple-element.54), channel_id=1, source_target_pairs={{1,0},{0,1},{3,2},{2,3},{5,4},{4,5},{7,6},{6,7},{9,8},{8,9},{11,10... | collective-permute-start | bytes 2949128 | tf_op jit(solution)/shard_map/ppermute | solution.py:891
  158.4 2.8 copy-start.4
  158.5 4.5 copy-start.21
  158.8 4.2 copy-start.10
  158.8 20.9 %copy-start.5 = (bf16[1,16,80,640]{3,2,1,0:T(8,128)(2,1)}, bf16[1,16,80,640]{3,2,1,0:T(8,128)(2,1)S(1)}, u32[]{:S(2)}) copy-start(bf16[1,16,80,640]{3,2,1,0:T(8,128)(2,1)S(1)} %get-tuple-element.90) | copy-start | bytes 4915204
  176.8 40.4 %collective-permute-start.4 = (bf16[384,1280]{1,0:T(8,128)(2,1)}, bf16[384,1280]{1,0:T(8,128)(2,1)}, u32[]{:S(2)}, u32[]{:S(2)}) collective-permute-start(bf16[384,1280]{1,0:T(8,128)(2,1)} %get-tuple-element.55), channel_id=1, source_target_pairs={{1,0},{0,1},{3,2},{2,3},{5,4},{4,5},{7,6},{6,7},{9,8},{8,9},{11,10... | collective-permute-start | bytes 2949128 | tf_op jit(solution)/shard_map/ppermute | solution.py:891
  179.2 3.0 copy-start
  273.0 0.7 copy-start.28
  273.0 0.7 copy-start.29
  273.0 0.7 copy-start.30
  273.0 0.8 copy-start.23
  273.0 0.8 copy-start.24
  273.0 0.8 copy-start.25
  274.5 4.6 copy-start.33
  274.5 44.4 %collective-permute-start.5 = (bf16[768,1280]{1,0:T(8,128)(2,1)}, bf16[768,1280]{1,0:T(8,128)(2,1)S(1)}, u32[]{:S(2)}, u32[]{:S(2)}) collective-permute-start(bf16[768,1280]{1,0:T(8,128)(2,1)} %fusion.24), channel_id=1, source_target_pairs={{1,0},{0,1},{3,2},{2,3},{5,4},{4,5},{7,6},{6,7},{9,8},{8,9},{11,10... | collective-permute-start | bytes 5898248 | tf_op jit(solution)/shard_map/ppermute | solution.py:891
  279.1 39.8 %copy-start.1 = (f32[768,1280]{1,0:T(8,128)S(1)}, f32[768,1280]{1,0:T(8,128)}, u32[]{:S(2)}) copy-start(f32[768,1280]{1,0:T(8,128)} %copy-done) | copy-start | bytes 11796484
  287.4 33.6 %copy-start.7 = (bf16[1,768,1280]{2,1,0:T(8,128)(2,1)S(1)}, bf16[1,768,1280]{2,1,0:T(8,128)(2,1)}, u32[]{:S(2)}) copy-start(bf16[1,768,1280]{2,1,0:T(8,128)(2,1)} %param.13) | copy-start | bytes 5898244
  321.0 3.5 copy-start.6
  326.0 22.4 %collective-permute-start.6 = (bf16[640,768]{1,0:T(8,128)(2,1)S(1)}, bf16[640,768]{1,0:T(8,128)(2,1)}, u32[]{:S(2)}, u32[]{:S(2)}) collective-permute-start(bf16[640,768]{1,0:T(8,128)(2,1)S(1)} %convolution_convert_fusion.6), channel_id=1, source_target_pairs={{1,0},{0,1},{3,2},{2,3},{5,4},{4,5},{7,6},{6,7},{9,8},{8,9},{11,10... | collective-permute-start | bytes 2949128 | tf_op jit(solution)/shard_map/ppermute | solution.py:891
  326.5 3.0 copy-start.22
  326.5 8.4 %slice-start = ((s8[6553600]{0:T(1024)(128)(4,1)}), s8[4194304]{0:T(1024)(128)(4,1)S(1)}, s32[]{:S(2)}) async-start(s8[6553600]{0:T(1024)(128)(4,1)} %bitcast.75), calls=%async_computation.4 | async-start | bytes 8388608
  326.5 8.3 %slice-start.2 = ((s8[7864320]{0:T(1024)(128)(4,1)}), s8[4194304]{0:T(1024)(128)(4,1)S(1)}, s32[]{:S(2)}) async-start(s8[7864320]{0:T(1024)(128)(4,1)} %bitcast.85), calls=%async_computation.6 | async-start | bytes 8388608
  329.4 2.9 copy-start.11
  329.4 5.4 %slice-start.1 = ((s8[6553600]{0:T(1024)(128)(4,1)}), s8[2359296]{0:T(1024)(128)(4,1)S(1)}, s32[]{:S(2)}) async-start(s8[6553600]{0:T(1024)(128)(4,1)} %bitcast.75), calls=%async_computation.5 | async-start | bytes 4718592
  329.4 5.4 %slice-start.3 = ((s8[7864320]{0:T(1024)(128)(4,1)}), s8[3670016]{0:T(1024)(128)(4,1)S(1)}, s32[]{:S(2)}) async-start(s8[7864320]{0:T(1024)(128)(4,1)} %bitcast.85), calls=%async_computation.7 | async-start | bytes 7340032
  399.5 108.4 %collective-permute-start.7 = (bf16[768,1280]{1,0:T(8,128)(2,1)}, bf16[768,1280]{1,0:T(8,128)(2,1)}, u32[]{:S(2)}, u32[]{:S(2)}) collective-permute-start(bf16[768,1280]{1,0:T(8,128)(2,1)} %fusion.18), channel_id=1, source_target_pairs={{1,0},{0,1},{3,2},{2,3},{5,4},{4,5},{7,6},{6,7},{9,8},{8,9},{11,10... | collective-permute-start | bytes 5898248 | tf_op jit(solution)/shard_map/ppermute | solution.py:891
  412.1 93.4 %copy-start.15 = (bf16[80,640]{1,0:T(8,128)(2,1)S(1)}, bf16[80,640]{1,0:T(8,128)(2,1)}, u32[]{:S(2)}) copy-start(bf16[80,640]{1,0:T(8,128)(2,1)} %param.15) | copy-start | bytes 307204
  412.1 93.5 %copy-start.16 = (bf16[80,640]{1,0:T(8,128)(2,1)S(1)}, bf16[80,640]{1,0:T(8,128)(2,1)}, u32[]{:S(2)}) copy-start(bf16[80,640]{1,0:T(8,128)(2,1)} %param.14) | copy-start | bytes 307204
  513.6 4.3 copy-start.8
  518.0 1.9 copy-start.20
  518.0 2.6 copy-start.19
  518.0 3.3 copy-start.18
  518.0 4.0 copy-start.17
Sparse Core Ops, SparseCore 0:
  10.3 104.0 all-gather.2
  116.7 63.6 all-gather.4
  273.2 150.9 reduce-scatter.1
